TPU v7x, 128 devices: a 2x2x16 block of a 8x8x16 slice. The times are simulated.
128 devices in a mesh: grp: 4 (over x, y), tok: 16 (over z), mdl: 2 (over core).
Axes of the slice: x: 2, y: 2, z: 16, core: 2. Of those that a mesh axis runs over, the one named last changes fastest.
The devices are a block of a 8x8x16 slice.
Arguments:
- hidden: bfloat16 [4096, 4096], P(('grp', 'tok'), 'mdl'), parts along dimension 0, may hold values from -3 to 3
- queries: bfloat16 [4096, 16, 128], P(('grp', 'tok'), 'mdl'), parts along dimension 0, may hold values from -8 to 8
- cache: bfloat16 [64, 2048, 4, 2, 128], P(('grp', 'tok'), None, 'mdl'), parts along dimension 0, may hold values from -8 to 8
- cache_lengths: int32 [64], P(('grp', 'tok')), parts along dimension 0, may hold values from 128 to 2048, as said below
- wkv: bfloat16 [4096, 4, 2, 128], P('tok', 'mdl'), may hold values from -0.09375 to 0.09375
- wo: bfloat16 [16, 128, 4096], P('mdl', None, 'tok'), may hold values from -0.5 to 0.5
- attn_gain: bfloat16 [4096], replicated, may hold values from 0.5 to 1.5
- moe_gain: bfloat16 [4096], replicated, may hold values from 0.5 to 1.5
- w_gate: bfloat16 [32, 4096, 896], P(('tok', 'mdl')), may hold values from -0.09375 to 0.09375
- w_up: bfloat16 [32, 4096, 896], P(('tok', 'mdl')), may hold values from -0.09375 to 0.09375
- w_down: bfloat16 [32, 896, 4096], P(('tok', 'mdl')), may hold values from -0.0625 to 0.0625
- expert_ids: int32 [4096, 2], P(('grp', 'tok', 'mdl')), parts along dimension 0, may hold values from 0 to 3, all different within a row; in each aligned block of 32 rows (0 to 31, 32 to 63, ...) at most 18 rows name the same one
- gates: float32 [4096, 2], P(('grp', 'tok', 'mdl')), parts along dimension 0, may hold values from 0.1 to 1
Outputs:
- mixed: bfloat16 [4096, 4096], P(('grp', 'tok', 'mdl')), parts along dimension 0
- fresh_key_value: bfloat16 [4096, 4, 2, 128], P(('grp', 'tok'), 'mdl'), parts along dimension 0
There are 4 independent parts, one for each index of `grp`. A program takes and returns all parts, laid end to end along the dimension named above; an argument that names none is the same for every part. Nothing has to cross between parts.
Inputs may be any that keep to these rules, and one draw needn't show every extreme that they name: `expert_ids`: each token names 2 different experts; in aligned blocks of 32 rows no expert is named by more than 18 rows, a bound that some block reaches. `cache_lengths`: some rollout holds exactly 2048 cached positions.
All inputs are finite; a program needn't handle non-finite values.
Results may differ from a plain program's by a relative error of at most 0.007.
Values may be sent and summed in bfloat16 or wider, within the bound.
A program may use at most 128 MiB of HBM per device.

v0:
```python
import math

import jax
import jax.numpy as jnp
from jax import lax
from jax.sharding import PartitionSpec as P

EXPERTS = 4
TOPK = 2


eps_norm = 1e-05
rope_base = 1000000.0
mask_fill = -1e30


def joined_along(tiles, dim):
    dims = list(tiles.shape[1:])
    dims[dim] *= tiles.shape[0]
    return jnp.moveaxis(tiles, 0, dim).reshape(dims)


def sent_to_all(shard, axis):
    copies = jnp.broadcast_to(shard, (lax.axis_size(axis), *shard.shape))
    return lax.all_to_all(copies, axis, split_axis=0, concat_axis=0, tiled=True)


def collect(shard, axis, dim):
    return joined_along(sent_to_all(shard, axis), dim)


def in_blocks(shard, dim, size):
    dims = shard.shape
    tiles = shard.reshape(*dims[:dim], size, dims[dim] // size, *dims[dim + 1 :])
    return jnp.moveaxis(tiles, dim, 0)


def sent_and_summed(shard, axis, dim):
    tiles = in_blocks(shard, dim, lax.axis_size(axis))
    arrived = lax.all_to_all(tiles, axis, split_axis=0, concat_axis=0, tiled=True)
    return arrived.sum(axis=0)


def sent_and_summed_2(shard, axis, dim):
    size = lax.axis_size(axis)
    tiles = lax.all_to_all(in_blocks(shard, dim, size), axis, 0, 0, tiled=True)
    return jnp.sum(tiles.astype(jnp.float32), axis=0)


def rms_scale(values_in, gain):
    values = values_in.astype(jnp.float32)
    meansq = jnp.mean(values * values, axis=-1, keepdims=True)
    return values * lax.rsqrt(meansq + eps_norm) * gain.astype(jnp.float32)


def rotate(key_rows, positions):
    half_dim = key_rows.shape[-1] // 2
    inverse = jnp.exp(
        jnp.arange(half_dim, dtype=jnp.float32) * (-2.0 * math.log(rope_base) / key_rows.shape[-1])
    )
    angle = positions.astype(jnp.float32)[:, None] * inverse[None, :]
    cosine = jnp.cos(angle)[:, None, :]
    sine_vals = jnp.sin(angle)[:, None, :]
    front_half = key_rows[..., :half_dim]
    back_half = key_rows[..., half_dim:]
    return jnp.concatenate(
        [front_half * cosine - back_half * sine_vals, back_half * cosine + front_half * sine_vals],
        axis=-1,
    )


def score_rows(query_rows, key_rows, scale_factor):
    return (
        lax.dot_general(
            query_rows, key_rows, (((1,), (1,)), ((), ())), preferred_element_type=jnp.float32
        )
        * scale_factor
    )


def head_attention(query_rows, cache_keys, cache_values, length, new_keys, new_values, head_group):
    row_count = query_rows.shape[0]
    block_len = min(512, cache_keys.shape[0])
    scale_factor = 1.0 / math.sqrt(query_rows.shape[1])
    token_of_row = jnp.arange(row_count) // head_group
    block_total = (length + block_len - 1) // block_len

    def block_scores(block_idx):
        row_offset = block_idx * block_len
        block_keys = lax.dynamic_slice_in_dim(cache_keys, row_offset, block_len, 0)
        allowed = row_offset + jnp.arange(block_len) < length
        return (
            jnp.where(
                allowed[None, :], score_rows(query_rows, block_keys, scale_factor), mask_fill
            ),
            allowed,
        )

    new_allowed = jnp.arange(new_keys.shape[0])[None, :] <= token_of_row[:, None]
    new_scores = jnp.where(new_allowed, score_rows(query_rows, new_keys, scale_factor), mask_fill)
    first_max = jnp.max(new_scores, axis=1)
    first_sum = jnp.sum(
        jnp.where(new_allowed, jnp.exp(new_scores - first_max[:, None]), 0.0), axis=1
    )

    def first_pass(block_idx, carry):
        run_max, run_sum = carry
        scores, allowed = block_scores(block_idx)
        next_max = jnp.maximum(run_max, jnp.max(scores, axis=1))
        weights = jnp.where(allowed[None, :], jnp.exp(scores - next_max[:, None]), 0.0)
        return (next_max, run_sum * jnp.exp(run_max - next_max) + jnp.sum(weights, axis=1))

    row_max, row_sum = lax.fori_loop(0, block_total, first_pass, (first_max, first_sum))
    new_probs = (
        jnp.where(new_allowed, jnp.exp(new_scores - row_max[:, None]), 0.0) / row_sum[:, None]
    ).astype(jnp.bfloat16)
    start_total = jnp.dot(new_probs, new_values, preferred_element_type=jnp.float32)

    def second_pass(block_idx, total):
        scores, allowed = block_scores(block_idx)
        probs = (
            jnp.where(allowed[None, :], jnp.exp(scores - row_max[:, None]), 0.0) / row_sum[:, None]
        ).astype(jnp.bfloat16)
        block_values = lax.dynamic_slice_in_dim(cache_values, block_idx * block_len, block_len, 0)
        return total + jnp.dot(probs, block_values, preferred_element_type=jnp.float32)

    total = lax.fori_loop(0, block_total, second_pass, start_total)
    return total.astype(jnp.bfloat16)


def shards(
    hidden,
    queries,
    cache,
    cache_lengths,
    wkv,
    wo,
    attn_gain,
    moe_gain,
    w_gate,
    w_up,
    w_down,
    expert_ids,
    gates,
):
    full_rows = collect(hidden, "mdl", 1)
    span_len = full_rows.shape[0]
    normalized_input = rms_scale(full_rows, attn_gain).astype(jnp.bfloat16)
    kv_heads = wkv.shape[1]
    head_dim = wkv.shape[3]
    weight_piece = lax.all_gather(wkv, "tok", axis=0, tiled=True)
    key_value_projection = jnp.dot(
        normalized_input,
        weight_piece.reshape(weight_piece.shape[0], -1),
        preferred_element_type=jnp.float32,
    ).reshape(span_len, kv_heads, 2, head_dim)
    length = cache_lengths[0]
    positions = length + jnp.arange(span_len, dtype=jnp.int32)
    fresh_key_value = jnp.stack(
        [rotate(key_value_projection[:, :, 0], positions), key_value_projection[:, :, 1]], axis=2
    ).astype(jnp.bfloat16)
    head_group = queries.shape[1] // kv_heads
    outputs = []
    for head_index in range(kv_heads):
        query_rows = queries[:, head_index * head_group : (head_index + 1) * head_group].reshape(
            span_len * head_group, head_dim
        )
        attended = head_attention(
            query_rows,
            cache[0, :, head_index, 0],
            cache[0, :, head_index, 1],
            length,
            fresh_key_value[:, head_index, 0],
            fresh_key_value[:, head_index, 1],
            head_group,
        )
        outputs.append(attended.reshape(span_len, head_group * head_dim))
    heads_out = jnp.concatenate(outputs, axis=1)
    weight_piece = lax.all_gather(wo, "tok", axis=2, tiled=True)
    attn_out = jnp.dot(
        heads_out,
        weight_piece.reshape(-1, weight_piece.shape[2]),
        preferred_element_type=jnp.float32,
    )
    core_rows = span_len // lax.axis_size("mdl")
    core_start = lax.axis_index("mdl") * core_rows
    attn_rows = sent_and_summed(attn_out, "mdl", 0)
    resid = (
        lax.dynamic_slice_in_dim(full_rows, core_start, core_rows, 0).astype(jnp.float32)
        + attn_rows
    )
    moe_in = rms_scale(resid, moe_gain).astype(jnp.bfloat16)
    expert_range = jnp.arange(EXPERTS)
    matches = expert_ids[:, :, None] == expert_range[None, None, :]
    chosen = jnp.sum(matches.astype(jnp.int32), axis=1)
    route = jnp.sum(jnp.where(matches, gates[:, :, None], 0.0), axis=1)
    slot_of = jnp.cumsum(chosen, axis=0) - chosen
    capacity = core_rows * TOPK * 9 // (8 * EXPERTS)
    slot_range = jnp.arange(capacity)
    select = (slot_of.T[:, None, :] == slot_range[None, :, None]) & (chosen.T[:, None, :] > 0)
    send_rows = jnp.einsum(
        "eci,id->ecd", select.astype(jnp.bfloat16), moe_in, preferred_element_type=jnp.float32
    ).astype(jnp.bfloat16)
    owners = lax.axis_size("tok") * lax.axis_size("mdl")
    slabs = owners // EXPERTS
    model_width = moe_in.shape[1]
    core_count = lax.axis_size("mdl")
    send_chip = jnp.repeat(send_rows, slabs // core_count, axis=0)
    received = lax.all_to_all(send_chip, "tok", split_axis=0, concat_axis=0, tiled=True)
    chip_count = received.shape[0]
    item_count = received.shape[1]
    both_cores = collect(received[:, None], "mdl", 1)
    received = both_cores.reshape(-1, item_count, model_width)
    flat_rows = received.reshape(-1, model_width)
    gate_val = jnp.dot(flat_rows, w_gate[0], preferred_element_type=jnp.float32)
    up_val = jnp.dot(flat_rows, w_up[0], preferred_element_type=jnp.float32)
    slab_hidden = (jax.nn.silu(gate_val) * up_val).astype(jnp.bfloat16)
    slab_out = jnp.dot(slab_hidden, w_down[0], preferred_element_type=jnp.float32).astype(
        jnp.bfloat16
    )
    slab_out = slab_out.reshape(received.shape)
    per_core = slab_out.reshape(chip_count, core_count, item_count, model_width).astype(jnp.float32)
    chip_total = sent_and_summed_2(per_core.astype(jnp.bfloat16), "mdl", 1)
    returned = lax.all_to_all(
        chip_total[:, 0].astype(jnp.bfloat16), "tok", split_axis=0, concat_axis=0, tiled=True
    ).astype(jnp.float32)
    summed = jnp.sum(returned.reshape(EXPERTS, slabs // core_count, capacity, model_width), axis=1)
    weight_table = select.astype(jnp.float32) * route.T[:, None, :]
    moe_out = jnp.einsum("eci,ecd->id", weight_table, summed, precision=lax.Precision.HIGHEST)
    mixed = (resid + moe_out).astype(jnp.bfloat16)
    return (mixed, fresh_key_value)


def solution(mesh):
    in_specs = (
        P(("grp", "tok"), "mdl"),
        P(("grp", "tok"), "mdl", None),
        P(("grp", "tok"), None, "mdl", None, None),
        P(("grp", "tok")),
        P("tok", "mdl", None, None),
        P("mdl", None, "tok"),
        P(),
        P(),
        P(("tok", "mdl"), None, None),
        P(("tok", "mdl"), None, None),
        P(("tok", "mdl"), None, None),
        P(("grp", "tok", "mdl"), None),
        P(("grp", "tok", "mdl"), None),
    )
    out_specs = (P(("grp", "tok", "mdl"), None), P(("grp", "tok"), "mdl", None, None))
    return jax.shard_map(shards, mesh=mesh, in_specs=in_specs, out_specs=out_specs, check_vma=False)
```

profile of v0, /device:TPU:69, one launch (start us, length us, event | category | flops | bytes accessed | tf_op | source)
XLA Modules:
  0.0 605.1 jit_solution(13349930791535107725)
XLA Ops:
  7.3 0.7 all-gather.3.cloned.1.call-update
  8.1 0.7 all-gather.5.cloned.1.call-update
  8.8 1.8 broadcast_in_dim.140
  10.6 13.4 %all-to-all-start = ((bf16[2,64,2048]{2,1,0:T(8,128)(2,1)}), bf16[2,64,2048]{2,1,0:T(8,128)(2,1)S(1)}, u32[]{:S(2)}, u32[]{:S(2)}) async-start(bf16[2,64,2048]{2,1,0:T(8,128)(2,1)} %broadcast_in_dim.140), calls=%async_computation | async-start | bytes 1048576 | tf_op jit(solution)/shard_map/all_to_all | solution.py:25
  24.7 0.7 reshape.191
  26.4 1.2 reshape.194
  28.3 3.0 fusion.112
  31.2 0.9 copy_bitcast_fusion.2
  32.3 50.2 %all-gather.3.cloned.1.call-done = bf16[4096,2,2,128]{3,2,1,0:T(2,128)(2,1)} async-done(((bf16[256,2,2,128]{3,2,1,0:T(2,128)(2,1)}), bf16[4096,2,2,128]{3,2,1,0:T(2,128)(2,1)}) %all-gather.3.cloned.1.call-update) | async-done | bytes 4194320 | tf_op jit(solution)/shard_map/all_gather | solution.py:151
  82.5 11.2 %copy.122 = bf16[4096,2,2,128]{0,3,2,1:T(8,128)(2,1)} copy(bf16[4096,2,2,128]{3,2,1,0:T(2,128)(2,1)} %all-gather.3.cloned.1.call-done) | data formatting | bytes 8388608 | tf_op jit(solution)/shard_map/reshape | solution.py:154
  93.7 3.6 fusion.116
  97.9 4.6 while.44
  97.9 0.7 add_compare_fusion.8
  99.1 0.7 add_compare_fusion.8
  102.7 8.6 %while.45 = (s32[]{:T(128)}, f32[256,128]{1,0:T(8,128)S(1)}, s32[]{:T(128)}, s32[]{:T(128)}, bf16[2048,128]{1,0:T(8,128)(2,1)S(1)}, /*index=5*/bf16[256,128]{1,0...) while((s32[]{:T(128)}, f32[256,128]{1,0:T(8,128)S(1)}, ...), condition=%wide.region_8.9_spmd, body=%wide.region_7.8_spmd.sunk | while | flops 67929096 | bytes 594099 | solution.py:127
  102.7 0.7 add_compare_fusion.9
  103.4 1.5 fusion.144
  104.9 0.7 add_compare_fusion.9
  105.5 1.4 fusion.144
  107.0 0.7 add_compare_fusion.9
  107.7 1.4 fusion.144
  109.1 0.7 add_compare_fusion.9
  109.8 1.4 fusion.144
  111.3 4.6 while.46
  111.4 0.7 add_compare_fusion.10
  112.5 0.7 add_compare_fusion.10
  113.7 0.7 add_compare_fusion.10
  116.1 4.9 while.47
  119.9 0.7 add_compare_fusion.11
  121.2 82.8 %all-gather.5.cloned.1.call-done = bf16[8,128,4096]{2,1,0:T(8,128)(2,1)} async-done(((bf16[8,128,256]{2,1,0:T(8,128)(2,1)}), bf16[8,128,4096]{2,1,0:T(8,128)(2,1)}) %all-gather.5.cloned.1.call-update) | async-done | bytes 8388624 | tf_op jit(solution)/shard_map/all_gather | solution.py:179
  203.9 5.0 fusion.80
  208.9 15.2 %all_to_all.30 = f32[2,32,4096]{2,1,0:T(8,128)S(1)} all-to-all(f32[2,32,4096]{2,1,0:T(8,128)S(1)} %fusion.80), channel_id=1, replica_groups=mesh['grp'=4,'tok'=16,'mdl'=2] {'mdl'}, dimensions={0} | all-to-all | bytes 2097152 | tf_op jit(solution)/shard_map/all_to_all | solution.py:40
  225.3 141.1 %all_to_all.31 = bf16[16,18,4096]{2,1,0:T(8,128)(2,1)S(1)} all-to-all(bf16[16,18,4096]{2,1,0:T(8,128)(2,1)S(1)} %bitcast.122), channel_id=1, replica_groups=mesh['grp'=4,'tok'=16,'mdl'=2] {'tok'}, dimensions={0} | all-to-all | bytes 4718592 | tf_op jit(solution)/shard_map/all_to_all | solution.py:209
  366.4 1.3 copy.114
  368.3 14.6 %all_to_all.32 = bf16[2,16,1,18,4096]{4,1,3,2,0:T(8,128)(2,1)S(1)} all-to-all(bf16[2,16,1,18,4096]{4,1,3,2,0:T(8,128)(2,1)S(1)} %broadcast_in_dim.146), channel_id=1, replica_groups=mesh['grp'=4,'tok'=16,'mdl'=2] {'mdl'}, dimensions={0} | all-to-all | bytes 9437184 | tf_op jit(solution)/shard_map/all_to_all | solution.py:25
  382.9 5.4 copy.115
  388.3 7.8 %reshape_reshape_reshape.3 = bf16[576,4096]{1,0:T(8,128)(2,1)} reshape(bf16[16,2,1,18,4096]{4,3,1,0,2:T(8,128)(2,1)} %copy.115) | data formatting | bytes 9437184 | tf_op jit(solution)/shard_map/reshape;reshape;reshape | solution.py:214
  396.1 10.7 %fusion.54 = f32[576,896]{1,0:T(8,128)S(1)} fusion(bf16[576,4096]{1,0:T(8,128)(2,1)} %reshape_reshape_reshape.3, bf16[1,4096,896]{2,1,0:T(8,128)(2,1)} %param.29), kind=kOutput, calls=%fused_computation.62 | convolution fusion | flops 4227858432 | bytes 14123008 | tf_op jit(solution)/shard_map/dot_general | solution.py:215
  406.8 17.4 %fusion.56 = bf16[576,4096]{1,0:T(8,128)(2,1)} fusion(bf16[1,896,4096]{2,1,0:T(8,128)(2,1)} %param.31, f32[576,896]{1,0:T(8,128)S(1)} %fusion.54, bf16[576,4096]{1,0:T(8,128)(2,1)} %reshape_reshape_reshape.3, bf16[1,4096,896]{2,1,0:T(8,128)(2,1)} %param.30), kind=kOutput, calls=%fused_computation.65 | convolution fusion | flops 8461172736 | bytes 26181632 | tf_op jit(solution)/shard_map/dot_general | solution.py:218
  424.3 7.6 %reshape.188 = bf16[16,2,1,18,4096]{4,3,1,0,2:T(8,128)(2,1)} reshape(bf16[576,4096]{1,0:T(8,128)(2,1)} %fusion.56) | data formatting | bytes 9437184 | tf_op jit(solution)/shard_map/reshape | solution.py:34
  431.9 5.4 copy.116
  437.2 8.6 %all_to_all.33 = bf16[2,16,1,18,4096]{4,1,3,2,0:T(8,128)(2,1)} all-to-all(bf16[2,16,1,18,4096]{4,1,3,2,0:T(8,128)(2,1)S(1)} %copy.116), channel_id=1, replica_groups=mesh['grp'=4,'tok'=16,'mdl'=2] {'mdl'}, dimensions={0} | all-to-all | bytes 9437184 | tf_op jit(solution)/shard_map/all_to_all | solution.py:46
  445.9 3.6 reduce_sum.109
  449.5 3.1 copy.117
  452.5 6.2 %all-to-all-start.5 = ((bf16[16,18,4096]{2,1,0:T(8,128)(2,1)}), bf16[16,18,4096]{2,1,0:T(8,128)(2,1)S(1)}, u32[]{:S(2)}, u32[]{:S(2)}) async-start(bf16[16,18,4096]{2,1,0:T(8,128)(2,1)} %copy.117), calls=%async_computation.5 | async-start | bytes 6291456 | tf_op jit(solution)/shard_map/all_to_all | solution.py:224
  458.8 0.7 copy.120
  459.5 135.9 %all-to-all-done.5 = bf16[16,18,4096]{2,1,0:T(8,128)(2,1)S(1)} async-done(((bf16[16,18,4096]{2,1,0:T(8,128)(2,1)}), bf16[16,18,4096]{2,1,0:T(8,128)(2,1)S(1)}, u32[]{:S(2)}, u32[]{:S(2)}) %all-to-all-start.5) | async-done | bytes 2359328 | tf_op jit(solution)/shard_map/all_to_all | solution.py:224
  596.6 1.6 fusion.60
  (113 shorter events, 15.5 us)
Async XLA Ops:
  7.2 20.5 %copy-start.8 = (s32[32,2]{0,1:T(2,128)S(1)}, s32[32,2]{0,1:T(2,128)}, u32[]{:S(2)}) copy-start(s32[32,2]{0,1:T(2,128)} %param.32) | copy-start | bytes 772
  7.2 20.7 %copy-start.7 = (bf16[4096]{0:T(1024)(128)(2,1)S(1)}, bf16[4096]{0:T(1024)(128)(2,1)}, u32[]{:S(2)}) copy-start(bf16[4096]{0:T(1024)(128)(2,1)} %param.28) | copy-start | bytes 24580
  7.2 21.0 %copy-start.6 = (bf16[64,8,128]{2,1,0:T(8,128)(2,1)S(1)}, bf16[64,8,128]{2,1,0:T(8,128)(2,1)}, u32[]{:S(2)}) copy-start(bf16[64,8,128]{2,1,0:T(8,128)(2,1)} %param.22) | copy-start | bytes 393220
  7.2 21.0 %copy-start.2 = (bf16[1,2048,2,2,128]{4,3,2,1,0:T(2,128)(2,1)S(1)}, bf16[1,2048,2,2,128]{4,3,2,1,0:T(2,128)(2,1)}, u32[]{:S(2)}) copy-start(bf16[1,2048,2,2,128]{4,3,2,1,0:T(2,128)(2,1)} %param.23) | copy-start | bytes 6291460
  7.2 75.3 %all-gather.3.cloned.1.call-start = ((), (), s32[]{:S(2)}) async-start(), calls=%async_computation.6 | async-start | bytes 4456448 | tf_op jit(solution)/shard_map/all_gather | solution.py:151
  8.0 195.9 %all-gather.5.cloned.1.call-start = ((), (), s32[]{:S(2)}) async-start(), calls=%async_computation.7 | async-start | bytes 8912896 | tf_op jit(solution)/shard_map/all_gather | solution.py:179
  10.6 14.8 %all-to-all-start = ((bf16[2,64,2048]{2,1,0:T(8,128)(2,1)}), bf16[2,64,2048]{2,1,0:T(8,128)(2,1)S(1)}, u32[]{:S(2)}, u32[]{:S(2)}) async-start(bf16[2,64,2048]{2,1,0:T(8,128)(2,1)} %broadcast_in_dim.140), calls=%async_computation | async-start | bytes 1048576 | tf_op jit(solution)/shard_map/all_to_all | solution.py:25
  27.7 196.8 %copy-start.3 = (bf16[2,8,8,2048]{3,2,0,1:T(8,128)(2,1)}, bf16[2,8,8,2048]{3,2,0,1:T(8,128)(2,1)S(1)}, u32[]{:S(2)}) copy-start(bf16[2,8,8,2048]{3,2,0,1:T(8,128)(2,1)S(1)} %copy.129) | copy-start | bytes 1572868
  32.3 61.4 %copy-start.5 = (bf16[64,4096,1,1]{1,0,2,3:T(8,128)(2,1)S(1)}, bf16[64,4096,1,1]{1,0,2,3:T(8,128)(2,1)}, u32[]{:S(2)}) copy-start(bf16[64,4096,1,1]{1,0,2,3:T(8,128)(2,1)} %reshape.194) | copy-start | bytes 1572868
  224.2 142.2 %copy-start = (f32[32,4096]{1,0:T(8,128)}, f32[32,4096]{1,0:T(8,128)S(1)}, u32[]{:S(2)}) copy-start(f32[32,4096]{1,0:T(8,128)S(1)} %reduce_sum.105) | copy-start | bytes 1572868
  449.4 9.3 %copy-start.9 = (f32[32,2]{0,1:T(2,128)S(1)}, f32[32,2]{0,1:T(2,128)}, u32[]{:S(2)}) copy-start(f32[32,2]{0,1:T(2,128)} %param.33) | copy-start | bytes 772
  452.5 142.9 %all-to-all-start.5 = ((bf16[16,18,4096]{2,1,0:T(8,128)(2,1)}), bf16[16,18,4096]{2,1,0:T(8,128)(2,1)S(1)}, u32[]{:S(2)}, u32[]{:S(2)}) async-start(bf16[16,18,4096]{2,1,0:T(8,128)(2,1)} %copy.117), calls=%async_computation.5 | async-start | bytes 6291456 | tf_op jit(solution)/shard_map/all_to_all | solution.py:224
  595.4 1.0 copy-start.1
  595.4 1.2 copy-start.4
Sparse Core Ops, SparseCore 0:
  9.7 72.7 all-gather.2
  84.1 119.7 all-gather.4
where the time goes:
time: 609 us; the launch traced here: 605 us
  waiting for transfers between devices  270 us (44%)
  blocking collectives  180 us (30%)
  local copies, waits for them, and re-layouts  52.8 us (9%)
  matrix products  49.6 us (8%)
  starting transfers between devices  19.7 us (3%)
  other arithmetic  17.3 us (3%)
  between operations  15.1 us (2%)
    all_to_all x1, blocking collectives, shards(): lax.all_to_all(send_chip, 'tok', split_axis=0, concat_axis=0, tiled=True)  141 us
    all_to_all x1, waiting for transfers between devices, shards(): lax.all_to_all(chip_total[:, 0].astype(jnp.bfloat16), 'tok', split_axis=0...  136 us
    all_gather x1, waiting for transfers between devices, shards(): weight_piece = lax.all_gather(wo, 'tok', axis=2, tiled=True)  82.8 us
    all_gather x1, waiting for transfers between devices, shards(): weight_piece = lax.all_gather(wkv, 'tok', axis=0, tiled=True)  50.2 us
    dot_general x1, matrix products, shards(): jnp.dot(slab_hidden, w_down[0], preferred_element_type=jnp.float32)  17.4 us
    all_to_all x1, blocking collectives, sent_and_summed(): lax.all_to_all(tiles, axis, split_axis=0, concat_axis=0, tiled=True)  15.2 us
    all_to_all x1, blocking collectives, sent_to_all(): return lax.all_to_all(copies, axis, split_axis=0, concat_axis=0, tiled=True)  14.6 us
    all_to_all x1, starting transfers between devices, sent_to_all(): return lax.all_to_all(copies, axis, split_axis=0, concat_axis=0, tiled=True)  13.4 us
  transfers between devices with their start and end apart: 4, of which 3 were waited for; matrix products, arithmetic and copies ran while one was open for 8% of the time, Pallas kernels for 0%

commit v1 on v0

--- a/solution.py
+++ b/solution.py
@@ -1,17 +1,23 @@
+import functools
 import math
 
 import jax
 import jax.numpy as jnp
 from jax import lax
+from jax.experimental import pallas as pl
+from jax.experimental.pallas import tpu as pltpu
 from jax.sharding import PartitionSpec as P
 
 EXPERTS = 4
 TOPK = 2
-
 
 eps_norm = 1e-05
 rope_base = 1000000.0
 mask_fill = -1e30
+
+MESH = pl.DeviceIdType.MESH
+bf16 = jnp.bfloat16
+f32 = jnp.float32
 
 
 def joined_along(tiles, dim):
@@ -39,12 +45,6 @@
     tiles = in_blocks(shard, dim, lax.axis_size(axis))
     arrived = lax.all_to_all(tiles, axis, split_axis=0, concat_axis=0, tiled=True)
     return arrived.sum(axis=0)
-
-
-def sent_and_summed_2(shard, axis, dim):
-    size = lax.axis_size(axis)
-    tiles = lax.all_to_all(in_blocks(shard, dim, size), axis, 0, 0, tiled=True)
-    return jnp.sum(tiles.astype(jnp.float32), axis=0)
 
 
 def rms_scale(values_in, gain):
@@ -126,6 +126,326 @@
 
     total = lax.fori_loop(0, block_total, second_pass, start_total)
     return total.astype(jnp.bfloat16)
+
+
+LANES = 128
+GT = 256
+DT = 512
+
+
+def expert_kernel(
+    half,
+    x_ref,
+    resid_ref,
+    wg_hbm,
+    wu_hbm,
+    wd_hbm,
+    out_ref,
+    xs,
+    wgu,
+    wd,
+    gu,
+    hid,
+    mine,
+    pout,
+    pin,
+    rsin,
+    wsem,
+    ag_send,
+    ag_recv,
+    x_send,
+    x_recv,
+    p_send,
+    p_recv,
+    rs_send,
+    rs_recv,
+):
+    ring = 2 * half
+    z = lax.axis_index("tok")
+    m = lax.axis_index("mdl")
+    ahead = lax.rem(z + 1, ring)
+    behind = lax.rem(z + ring - 1, ring)
+    partner = {"mdl": 1 - m}
+    expert = z // (ring // EXPERTS)
+    block, width = resid_ref.shape
+    ffs = wg_hbm.shape[1]
+    wide = x_ref.shape[1]
+    cut = width // 2
+    spans = ((0, cut), (cut, wide - cut))
+    ospans = ((0, cut), (cut, width - cut))
+
+    loads = (
+        pltpu.make_async_copy(wg_hbm, wgu.at[:, pl.ds(0, ffs)], wsem.at[0]),
+        pltpu.make_async_copy(wu_hbm, wgu.at[:, pl.ds(ffs, ffs)], wsem.at[1]),
+        pltpu.make_async_copy(wd_hbm, wd, wsem.at[2]),
+    )
+
+    barrier = pltpu.get_barrier_semaphore()
+    for who in ({"tok": ahead}, {"tok": behind}, partner):
+        pl.semaphore_signal(barrier, inc=1, device_id=who, device_id_type=MESH)
+    pl.semaphore_wait(barrier, 3)
+
+    def ring_copy(src, dst_slot, flow, piece, step):
+        lo, size = spans[piece]
+        return pltpu.make_async_remote_copy(
+            src_ref=src.at[:, pl.ds(lo, size)],
+            dst_ref=xs.at[dst_slot, 0, :, pl.ds(lo, size)],
+            send_sem=ag_send.at[step, flow, piece],
+            recv_sem=ag_recv.at[step, flow, piece],
+            device_id={"tok": behind if flow == 0 else ahead},
+            device_id_type=MESH,
+        )
+
+    def partner_copy(src, slot, piece):
+        lo, size = spans[piece]
+        return pltpu.make_async_remote_copy(
+            src_ref=src.at[:, pl.ds(lo, size)],
+            dst_ref=xs.at[slot, 1, :, pl.ds(lo, size)],
+            send_sem=x_send.at[slot, piece],
+            recv_sem=x_recv.at[slot, piece],
+            device_id=partner,
+            device_id_type=MESH,
+        )
+
+    def first_slot(flow, piece):
+        return 2 + flow if half > 1 else 1
+
+    for piece in range(2):
+        for flow in range(2):
+            ring_copy(x_ref, 2 + flow, flow, piece, 1).start()
+    for load in loads:
+        load.start()
+    for piece in range(2):
+        partner_copy(x_ref, 0, piece).start()
+    xs[0, 0] = x_ref[...]
+
+    def gate_up(g, lo, hi):
+        def tile(n, carry):
+            cols = pl.ds(pl.multiple_of(n * GT, GT), GT)
+            rows = xs[pl.ds(2 * g, 2), :, :, pl.ds(0, width)].reshape(4 * block, width)
+            gu[:, cols] = jnp.dot(rows, wgu[:, cols], preferred_element_type=f32)
+            return carry
+
+        lax.fori_loop(lo, hi, tile, 0)
+
+    def activate():
+        gate = gu[:, pl.ds(0, ffs)]
+        up = gu[:, pl.ds(ffs, ffs)]
+        hid[...] = (gate / (1.0 + jnp.exp(-gate)) * up).astype(bf16)
+
+    def weight_of(g):
+        tail = xs[pl.ds(2 * g, 2), :, :, pl.ds(width, LANES)].reshape(4 * block, LANES)
+        lane = lax.broadcasted_iota(jnp.int32, (4 * block, LANES), 1)
+        pick = (lane == expert) | (lane == expert + EXPERTS)
+        return jnp.sum(jnp.where(pick, tail.astype(f32), 0.0), axis=1, keepdims=True)
+
+    def down(g, lo, hi):
+        weight = weight_of(g)
+
+        def tile(n, carry):
+            cols = pl.ds(pl.multiple_of(n * DT, DT), DT)
+            got = jnp.dot(hid[...], wd[:, cols], preferred_element_type=f32) * weight
+            got = got.astype(bf16)
+            for slot in range(2):
+                mine[2 * g + slot, :, cols] = got[2 * slot * block : (2 * slot + 1) * block]
+                pout[2 * g + slot, :, cols] = got[(2 * slot + 1) * block : (2 * slot + 2) * block]
+            return carry
+
+        lax.fori_loop(lo, hi, tile, 0)
+
+    gtiles = 2 * ffs // GT
+    dtiles = width // DT
+
+    def give(g):
+        return pltpu.make_async_remote_copy(
+            src_ref=pout.at[pl.ds(2 * g, 2)],
+            dst_ref=pin.at[pl.ds(2 * g, 2)],
+            send_sem=p_send.at[g],
+            recv_sem=p_recv.at[g],
+            device_id=partner,
+            device_id_type=MESH,
+        )
+
+    def await_partner(g):
+        for slot in range(2):
+            for piece in range(2):
+                partner_copy(x_ref, 2 * g + slot, piece).wait_recv()
+
+    def arrive(s, flow, piece, onward):
+        ring_copy(x_ref, 2 * s + flow, flow, piece, s).wait_recv()
+        if onward is not None:
+            ring_copy(xs.at[2 * s + flow, 0], onward, flow, piece, s + 1).start()
+        partner_copy(xs.at[2 * s + flow, 0], 2 * s + flow, piece).start()
+
+    def first_part(g):
+        await_partner(g)
+        gate_up(g, 0, gtiles)
+
+    def second_part(g):
+        activate()
+        down(g, 0, dtiles)
+        give(g).start()
+
+    for flow in range(2):
+        arrive(1, flow, 0, 4 + flow)
+    for load in loads:
+        load.wait()
+    for flow in range(2):
+        arrive(1, flow, 1, 4 + flow)
+
+    def body(s, carry):
+        for flow in range(2):
+            arrive(s, flow, 0, 2 * (s + 1) + flow)
+        first_part(s - 1)
+        for flow in range(2):
+            arrive(s, flow, 1, 2 * (s + 1) + flow)
+        second_part(s - 1)
+        return carry
+
+    lax.fori_loop(2, half - 1, body, 0)
+
+    last = half - 1
+    arrive(last, 0, 0, 1)
+    arrive(last, 1, 0, None)
+    first_part(last - 1)
+    arrive(last, 0, 1, None)
+    arrive(last, 1, 1, 1)
+    second_part(last - 1)
+
+    await_partner(last)
+    gate_up(last, 0, gtiles)
+    for flow in range(2):
+        ring_copy(x_ref, 1, flow, flow, half).wait_recv()
+        partner_copy(xs.at[1, 0], 1, flow).start()
+    second_part(last)
+    await_partner(0)
+    gate_up(0, 0, gtiles)
+    activate()
+    down(0, 0, dtiles)
+    give(0).start()
+
+    def sum_copy(slot, flow, piece, step):
+        lo, size = ospans[piece]
+        return pltpu.make_async_remote_copy(
+            src_ref=mine.at[slot, :, pl.ds(lo, size)],
+            dst_ref=rsin.at[flow, step, :, pl.ds(lo, size)],
+            send_sem=rs_send.at[step, flow, piece],
+            recv_sem=rs_recv.at[step, flow, piece],
+            device_id={"tok": ahead if flow == 0 else behind},
+            device_id_type=MESH,
+        )
+
+    def add_and_send(slot, flow, piece, step, incoming):
+        lo, size = ospans[piece]
+        cols = pl.ds(lo, size)
+        total = mine[slot, :, cols].astype(f32) + pin[slot, :, cols].astype(f32)
+        if incoming:
+            sum_copy(slot, flow, piece, step - 1).wait_recv()
+            total = total + rsin[flow, step - 1, :, cols].astype(f32)
+        mine[slot, :, cols] = total.astype(bf16)
+        sum_copy(slot, flow, piece, step).start()
+
+    give(0).wait_recv()
+    for flow in range(2):
+        add_and_send(1, flow, flow, 0, False)
+    give(last).wait_recv()
+    for flow in range(2):
+        add_and_send(2 * last + flow, flow, 1 - flow, 1, False)
+    for flow in range(2):
+        add_and_send(2 * last + flow, flow, flow, 1, True)
+
+    def fold(step, carry):
+        s = half - step
+        give(s).wait_recv()
+        for piece in range(2):
+            for flow in range(2):
+                add_and_send(2 * s + flow, flow, piece, step, True)
+        return carry
+
+    lax.fori_loop(2, half, fold, 0)
+
+    for piece in range(2):
+        lo, size = ospans[piece]
+        cols = pl.ds(lo, size)
+        total = resid_ref[:, cols] + mine[0, :, cols].astype(f32) + pin[0, :, cols].astype(f32)
+        for flow in range(2):
+            sum_copy(0, flow, piece, half - 1).wait_recv()
+            total = total + rsin[flow, half - 1, :, cols].astype(f32)
+        out_ref[:, cols] = total.astype(bf16)
+
+    def drain_ring(s, carry):
+        for flow in range(2):
+            for piece in range(2):
+                ring_copy(x_ref, 1, flow, piece, s).wait_send()
+        return carry
+
+    lax.fori_loop(1, half, drain_ring, 0)
+    for flow in range(2):
+        ring_copy(x_ref, 1, flow, flow, half).wait_send()
+
+    def drain_slots(slot, carry):
+        for piece in range(2):
+            partner_copy(x_ref, slot, piece).wait_send()
+        return carry
+
+    lax.fori_loop(0, ring, drain_slots, 0)
+
+    def drain_groups(g, carry):
+        give(g).wait_send()
+        return carry
+
+    lax.fori_loop(0, half, drain_groups, 0)
+
+    def drain_sums(step, carry):
+        for flow in range(2):
+            for piece in range(2):
+                sum_copy(0, flow, piece, step).wait_send()
+        return carry
+
+    for flow in range(2):
+        sum_copy(0, flow, flow, 0).wait_send()
+    lax.fori_loop(1, half, drain_sums, 0)
+
+
+def expert_layer(x_wide, resid, w_gate, w_up, w_down):
+    ring = lax.axis_size("tok")
+    half = ring // 2
+    block, width = resid.shape
+    ffs = w_gate.shape[1]
+    wide = x_wide.shape[1]
+    vmem = pl.BlockSpec(memory_space=pltpu.VMEM)
+    hbm = pl.BlockSpec(memory_space=pl.ANY)
+    dma = pltpu.SemaphoreType.DMA
+    return pl.pallas_call(
+        functools.partial(expert_kernel, half),
+        out_shape=jax.ShapeDtypeStruct((block, width), bf16),
+        in_specs=[vmem, vmem, hbm, hbm, hbm],
+        out_specs=vmem,
+        scratch_shapes=[
+            pltpu.VMEM((ring, 2, block, wide), bf16),
+            pltpu.VMEM((width, 2 * ffs), bf16),
+            pltpu.VMEM((ffs, width), bf16),
+            pltpu.VMEM((4 * block, 2 * ffs), f32),
+            pltpu.VMEM((4 * block, ffs), bf16),
+            pltpu.VMEM((ring, block, width), bf16),
+            pltpu.VMEM((ring, block, width), bf16),
+            pltpu.VMEM((ring, block, width), bf16),
+            pltpu.VMEM((2, half, block, width), bf16),
+            dma((3,)),
+            dma((half + 1, 2, 2)),
+            dma((half + 1, 2, 2)),
+            dma((ring, 2)),
+            dma((ring, 2)),
+            dma((half,)),
+            dma((half,)),
+            dma((half, 2, 2)),
+            dma((half, 2, 2)),
+        ],
+        compiler_params=pltpu.CompilerParams(
+            collective_id=1, has_side_effects=True, vmem_limit_bytes=67043328
+        ),
+        name="expert_layer",
+    )(x_wide, resid, w_gate, w_up, w_down)
 
 
 def shards(
@@ -190,44 +510,13 @@
         + attn_rows
     )
     moe_in = rms_scale(resid, moe_gain).astype(jnp.bfloat16)
-    expert_range = jnp.arange(EXPERTS)
-    matches = expert_ids[:, :, None] == expert_range[None, None, :]
-    chosen = jnp.sum(matches.astype(jnp.int32), axis=1)
+    matches = expert_ids[:, :, None] == jnp.arange(EXPERTS)[None, None, :]
     route = jnp.sum(jnp.where(matches, gates[:, :, None], 0.0), axis=1)
-    slot_of = jnp.cumsum(chosen, axis=0) - chosen
-    capacity = core_rows * TOPK * 9 // (8 * EXPERTS)
-    slot_range = jnp.arange(capacity)
-    select = (slot_of.T[:, None, :] == slot_range[None, :, None]) & (chosen.T[:, None, :] > 0)
-    send_rows = jnp.einsum(
-        "eci,id->ecd", select.astype(jnp.bfloat16), moe_in, preferred_element_type=jnp.float32
-    ).astype(jnp.bfloat16)
-    owners = lax.axis_size("tok") * lax.axis_size("mdl")
-    slabs = owners // EXPERTS
-    model_width = moe_in.shape[1]
-    core_count = lax.axis_size("mdl")
-    send_chip = jnp.repeat(send_rows, slabs // core_count, axis=0)
-    received = lax.all_to_all(send_chip, "tok", split_axis=0, concat_axis=0, tiled=True)
-    chip_count = received.shape[0]
-    item_count = received.shape[1]
-    both_cores = collect(received[:, None], "mdl", 1)
-    received = both_cores.reshape(-1, item_count, model_width)
-    flat_rows = received.reshape(-1, model_width)
-    gate_val = jnp.dot(flat_rows, w_gate[0], preferred_element_type=jnp.float32)
-    up_val = jnp.dot(flat_rows, w_up[0], preferred_element_type=jnp.float32)
-    slab_hidden = (jax.nn.silu(gate_val) * up_val).astype(jnp.bfloat16)
-    slab_out = jnp.dot(slab_hidden, w_down[0], preferred_element_type=jnp.float32).astype(
-        jnp.bfloat16
-    )
-    slab_out = slab_out.reshape(received.shape)
-    per_core = slab_out.reshape(chip_count, core_count, item_count, model_width).astype(jnp.float32)
-    chip_total = sent_and_summed_2(per_core.astype(jnp.bfloat16), "mdl", 1)
-    returned = lax.all_to_all(
-        chip_total[:, 0].astype(jnp.bfloat16), "tok", split_axis=0, concat_axis=0, tiled=True
-    ).astype(jnp.float32)
-    summed = jnp.sum(returned.reshape(EXPERTS, slabs // core_count, capacity, model_width), axis=1)
-    weight_table = select.astype(jnp.float32) * route.T[:, None, :]
-    moe_out = jnp.einsum("eci,ecd->id", weight_table, summed, precision=lax.Precision.HIGHEST)
-    mixed = (resid + moe_out).astype(jnp.bfloat16)
+    high = route.astype(bf16)
+    low = (route - high.astype(f32)).astype(bf16)
+    pad = jnp.zeros((core_rows, LANES - 2 * EXPERTS), bf16)
+    x_wide = jnp.concatenate([moe_in, high, low, pad], axis=1)
+    mixed = expert_layer(x_wide, resid, w_gate[0], w_up[0], w_down[0])
     return (mixed, fresh_key_value)
 
 

time: 609 us -> 349 us (0.57)
  blocking collectives: 180 us -> 14.5 us
  waiting for transfers between devices: 270 us -> 149 us
  Pallas kernels: 0 us -> 113 us
  matrix products: 49.6 us -> 11.8 us
  local copies, waits for them, and re-layouts: 52.8 us -> 25.8 us
  other arithmetic: 17.3 us -> 5 us
  starting transfers between devices: 19.7 us -> 13.5 us
    all_to_all x3 -> x0, blocking collectives: 164 us -> none  [the longest x1 141 us: shards(): lax.all_to_all(send_chip, 'tok', split_axis=0, concat_axis=0, tiled=True)]
    all_to_all x1 -> x0, waiting for transfers between devices: 136 us -> none  [shards(): lax.all_to_all(chip_total[:, 0].astype(jnp.bfloat16), 'tok', split_axis=0...]
    pallas_call x0 -> x1, Pallas kernels: none -> 113 us  [expert_layer(): pl.pallas_call(functools.partial(expert_kernel, half), out_shape=jax.Shap...]
    dot_general x4 -> x0, matrix products: 30.2 us -> none  [the longest x1 17.4 us: shards(): jnp.dot(slab_hidden, w_down[0], preferred_element_type=jnp.float32)]
    all_gather x1, waiting for transfers between devices: 82.8 us -> 99.7 us  [shards(): weight_piece = lax.all_gather(wo, 'tok', axis=2, tiled=True)]
    transpose x2 -> x0, local copies, waits for them, and re-layouts: 10.8 us -> none  [the longest x1 5.39 us: joined_along(): return jnp.moveaxis(tiles, 0, dim).reshape(dims)]
    lt x16 -> x4, other arithmetic: 10.5 us -> 2.61 us  [block_scores(): allowed = row_offset + jnp.arange(block_len) < length]
    another operation x1 -> x0, local copies, waits for them, and re-layouts: 7.79 us -> none  [shards(): flat_rows = received.reshape(-1, model_width)]
  transfers between devices with their start and end apart: 4 -> 3, of which waited for: 3 -> 2; matrix products, arithmetic and copies ran while one was open for 8% -> 10% of each run, Pallas kernels for 0% -> 0%
where the time goes in v1:
time: 349 us; the launch traced here: 348 us
  waiting for transfers between devices  149 us (43%)
  Pallas kernels  113 us (32%)
  local copies, waits for them, and re-layouts  25.8 us (7%)
  between operations  15 us (4%)
  blocking collectives  14.5 us (4%)
  starting transfers between devices  13.5 us (4%)
  matrix products  11.8 us (3%)
  other arithmetic  5 us (1%)
    pallas_call x1, Pallas kernels, expert_layer(): pl.pallas_call(functools.partial(expert_kernel, half), out_shape=jax.Shap...  113 us
    all_gather x1, waiting for transfers between devices, shards(): weight_piece = lax.all_gather(wo, 'tok', axis=2, tiled=True)  99.7 us
    all_gather x1, waiting for transfers between devices, shards(): weight_piece = lax.all_gather(wkv, 'tok', axis=0, tiled=True)  47.7 us
    all_to_all x1, blocking collectives, sent_and_summed(): lax.all_to_all(tiles, axis, split_axis=0, concat_axis=0, tiled=True)  14.5 us
    all_to_all x1, starting transfers between devices, sent_to_all(): return lax.all_to_all(copies, axis, split_axis=0, concat_axis=0, tiled=True)  13.4 us
    reshape x1, local copies, waits for them, and re-layouts, shards(): weight_piece.reshape(weight_piece.shape[0], -1)  11.2 us
  transfers between devices with their start and end apart: 3, of which 2 were waited for; matrix products, arithmetic and copies ran while one was open for 10% of the time, Pallas kernels for 0%

profile of v1, /device:TPU:69, one launch (start us, length us, event | category | flops | bytes accessed | tf_op | source)
XLA Modules:
  0.0 347.9 jit_solution(1485435756300752945)
XLA Ops:
  7.3 0.7 all-gather.3.cloned.1.call-update
  8.1 0.7 all-gather.5.cloned.1.call-update
  8.8 1.8 broadcast_in_dim.132
  10.6 13.4 %all-to-all-start = ((bf16[2,64,2048]{2,1,0:T(8,128)(2,1)}), bf16[2,64,2048]{2,1,0:T(8,128)(2,1)S(1)}, u32[]{:S(2)}, u32[]{:S(2)}) async-start(bf16[2,64,2048]{2,1,0:T(8,128)(2,1)} %broadcast_in_dim.132), calls=%async_computation | async-start | bytes 1048576 | tf_op jit(solution)/shard_map/all_to_all | solution.py:31
  24.7 0.7 select_reduce_fusion.4
  25.6 0.1 copy.66
  25.7 0.7 reshape.168
  26.4 0.2 fusion.56
  26.6 0.2 fusion.58
  26.8 1.4 copy.57
  28.2 1.4 reshape.169
  29.6 0.8 copy.75
  30.5 0.2 multiply_cosine_fusion
  30.8 3.0 fusion.79
  33.8 0.9 copy_bitcast_fusion.2
  34.7 0.1 copy_bitcast_fusion
  34.9 47.7 %all-gather.3.cloned.1.call-done = bf16[4096,2,2,128]{3,2,1,0:T(2,128)(2,1)} async-done(((bf16[256,2,2,128]{3,2,1,0:T(2,128)(2,1)}), bf16[4096,2,2,128]{3,2,1,0:T(2,128)(2,1)}) %all-gather.3.cloned.1.call-update) | async-done | bytes 4194320 | tf_op jit(solution)/shard_map/all_gather | solution.py:471
  82.5 11.2 %copy.69 = bf16[4096,2,2,128]{0,3,2,1:T(8,128)(2,1)} copy(bf16[4096,2,2,128]{3,2,1,0:T(2,128)(2,1)} %all-gather.3.cloned.1.call-done) | data formatting | bytes 8388608 | tf_op jit(solution)/shard_map/reshape | solution.py:474
  93.7 3.6 %fusion.83 = (bf16[64,2,2,128]{3,0,2,1:T(8,128)(2,1)S(1)}, f32[64,2,2,128]{3,0,2,1:T(8,128)S(1)}) fusion(bf16[4096,2,2,128]{0,3,2,1:T(8,128)(2,1)} %copy.69, bf16[64,4096,1,1]{1,0,2,3:T(8,128)(2,1)S(1)} %reshape.169), kind=kOutput, calls=%fused_computation.129 | convolution fusion | flops 268468224 | bytes 4915200 | tf_op jit(solution)/shard_map/dot_general | solution.py:472
  97.5 0.2 fusion.82
  97.7 0.2 fusion.81
  97.9 1.1 while.44
  97.9 0.7 add_compare_fusion.8
  98.6 0.3 fusion.104
  98.9 0.2 select_reduce_fusion.7
  99.1 0.2 fusion.64
  99.3 2.1 while.45
  99.3 0.7 add_compare_fusion.9
  100.0 1.4 fusion.108
  101.5 1.1 while.46
  101.5 0.7 add_compare_fusion.10
  102.2 0.3 fusion.110
  102.5 0.2 select_reduce_fusion.8
  102.7 0.2 fusion.65
  102.9 1.2 while.47
  102.9 0.7 add_compare_fusion.11
  103.5 0.5 fusion.114
  104.2 0.7 copy.67
  104.9 99.7 %all-gather.5.cloned.1.call-done = bf16[8,128,4096]{2,1,0:T(8,128)(2,1)} async-done(((bf16[8,128,256]{2,1,0:T(8,128)(2,1)}), bf16[8,128,4096]{2,1,0:T(8,128)(2,1)}) %all-gather.5.cloned.1.call-update) | async-done | bytes 8388624 | tf_op jit(solution)/shard_map/all_gather | solution.py:499
  204.6 5.0 %fusion.60 = f32[2,32,4096]{2,1,0:T(8,128)S(1)} fusion(bf16[1024,4096,1]{1,0,2:T(8,128)(2,1)} %bitcast.83, bf16[2,32,512]{2,1,0:T(8,128)(2,1)S(1)} %concatenate.17, bf16[2,32,512]{2,1,0:T(8,128)(2,1)S(1)} %concatenate.16), kind=kOutput, calls=%fused_computation.79 | convolution fusion | flops 537133056 | bytes 9568256 | tf_op jit(solution)/shard_map/dot_general | solution.py:500
  209.6 14.5 %all_to_all.10 = f32[2,32,4096]{2,1,0:T(8,128)S(1)} all-to-all(f32[2,32,4096]{2,1,0:T(8,128)S(1)} %fusion.60), channel_id=1, replica_groups=mesh['grp'=4,'tok'=16,'mdl'=2] {'mdl'}, dimensions={0} | all-to-all | bytes 2097152 | tf_op jit(solution)/shard_map/all_to_all | solution.py:46
  224.1 0.1 reduce_sum.75
  224.2 0.2 multiply_reduce_fusion
  224.4 0.8 copy-done.1
  225.2 0.1 multiply_convert_fusion
  225.3 0.8 concatenate.19.x_ref
  226.1 113.3 %expert_layer.1 = bf16[32,4096]{1,0:T(8,128)(2,1)} custom-call(bf16[32,4224]{1,0:T(8,128)(2,1)} %concatenate.19.x_ref, f32[32,4096]{1,0:T(8,128)} %copy-done.1, bf16[4096,896]{1,0:T(8,128)(2,1)} %bitcast.85, bf16[4096,896]{1,0:T(8,128)(2,1)} %bitcast.86, bf16[896,4096]{1,0:T(8,128)(2,1)} %bitcast.87), custom_call_target="tpu_custom_call" | custom-call | tf_op jit(solution)/shard_map/expert_layer/pallas_call | solution.py:419
  339.4 1.7 copy.112
  (40 shorter events, 0.8 us)
Async XLA Ops:
  7.2 23.3 %copy-start.4 = (bf16[4096]{0:T(1024)(128)(2,1)S(1)}, bf16[4096]{0:T(1024)(128)(2,1)}, u32[]{:S(2)}) copy-start(bf16[4096]{0:T(1024)(128)(2,1)} %param.28) | copy-start | bytes 24580
  7.2 23.5 %copy-start.3 = (bf16[64,8,128]{2,1,0:T(8,128)(2,1)S(1)}, bf16[64,8,128]{2,1,0:T(8,128)(2,1)}, u32[]{:S(2)}) copy-start(bf16[64,8,128]{2,1,0:T(8,128)(2,1)} %param.22) | copy-start | bytes 393220
  7.2 23.6 %copy-start = (bf16[1,2048,2,2,128]{4,3,2,1,0:T(2,128)(2,1)S(1)}, bf16[1,2048,2,2,128]{4,3,2,1,0:T(2,128)(2,1)}, u32[]{:S(2)}) copy-start(bf16[1,2048,2,2,128]{4,3,2,1,0:T(2,128)(2,1)} %param.23) | copy-start | bytes 6291460
  7.2 75.3 %all-gather.3.cloned.1.call-start = ((), (), s32[]{:S(2)}) async-start(), calls=%async_computation.2 | async-start | bytes 4456448 | tf_op jit(solution)/shard_map/all_gather | solution.py:471
  8.0 196.6 %all-gather.5.cloned.1.call-start = ((), (), s32[]{:S(2)}) async-start(), calls=%async_computation.3 | async-start | bytes 8912896 | tf_op jit(solution)/shard_map/all_gather | solution.py:499
  10.6 15.8 %all-to-all-start = ((bf16[2,64,2048]{2,1,0:T(8,128)(2,1)}), bf16[2,64,2048]{2,1,0:T(8,128)(2,1)S(1)}, u32[]{:S(2)}, u32[]{:S(2)}) async-start(bf16[2,64,2048]{2,1,0:T(8,128)(2,1)} %broadcast_in_dim.132), calls=%async_computation | async-start | bytes 1048576 | tf_op jit(solution)/shard_map/all_to_all | solution.py:31
  104.1 120.0 %copy-start.2 = (bf16[2,8,8,2048]{3,2,0,1:T(8,128)(2,1)S(1)}, bf16[2,8,8,2048]{3,2,0,1:T(8,128)(2,1)}, u32[]{:S(2)}) copy-start(bf16[2,8,8,2048]{3,2,0,1:T(8,128)(2,1)} %copy.75) | copy-start | bytes 1572868
  224.4 0.8 copy-start.1
Sparse Core Ops, SparseCore 0:
  9.7 72.7 all-gather.2
  84.1 120.4 all-gather.4

commit v2 on v1

--- a/solution.py
+++ b/solution.py
@@ -20,115 +20,496 @@
 f32 = jnp.float32
 
 
-def joined_along(tiles, dim):
-    dims = list(tiles.shape[1:])
-    dims[dim] *= tiles.shape[0]
-    return jnp.moveaxis(tiles, 0, dim).reshape(dims)
-
-
-def sent_to_all(shard, axis):
-    copies = jnp.broadcast_to(shard, (lax.axis_size(axis), *shard.shape))
-    return lax.all_to_all(copies, axis, split_axis=0, concat_axis=0, tiled=True)
-
-
-def collect(shard, axis, dim):
-    return joined_along(sent_to_all(shard, axis), dim)
-
-
-def in_blocks(shard, dim, size):
-    dims = shard.shape
-    tiles = shard.reshape(*dims[:dim], size, dims[dim] // size, *dims[dim + 1 :])
-    return jnp.moveaxis(tiles, dim, 0)
-
-
-def sent_and_summed(shard, axis, dim):
-    tiles = in_blocks(shard, dim, lax.axis_size(axis))
-    arrived = lax.all_to_all(tiles, axis, split_axis=0, concat_axis=0, tiled=True)
-    return arrived.sum(axis=0)
-
-
-def rms_scale(values_in, gain):
-    values = values_in.astype(jnp.float32)
-    meansq = jnp.mean(values * values, axis=-1, keepdims=True)
-    return values * lax.rsqrt(meansq + eps_norm) * gain.astype(jnp.float32)
-
-
-def rotate(key_rows, positions):
-    half_dim = key_rows.shape[-1] // 2
-    inverse = jnp.exp(
-        jnp.arange(half_dim, dtype=jnp.float32) * (-2.0 * math.log(rope_base) / key_rows.shape[-1])
+LANES = 128
+KEYS = 512
+
+
+def permutation(groups, size):
+    each = size // groups
+    row = lax.broadcasted_iota(jnp.int32, (size, size), 0)
+    col = lax.broadcasted_iota(jnp.int32, (size, size), 1)
+    return jnp.where(col == lax.rem(row, each) * groups + row // each, 1.0, 0.0).astype(bf16)
+
+
+def prelude_kernel(
+    half,
+    side,
+    hid_ref,
+    q_ref,
+    cache_hbm,
+    len_ref,
+    wkv_ref,
+    wo_ref,
+    again_ref,
+    mgain_ref,
+    ids_ref,
+    gates_ref,
+    x_ref,
+    resid_ref,
+    fresh_ref,
+    hfull,
+    normed,
+    kvbuf,
+    wobuf,
+    raw,
+    keys,
+    vals,
+    qs,
+    kvacc,
+    smax,
+    ssum,
+    sacc,
+    heads,
+    part,
+    part_in,
+    csem,
+    h_send,
+    h_recv,
+    kv_send,
+    kv_recv,
+    kvn_send,
+    kvn_recv,
+    wo_send,
+    wo_recv,
+    won_send,
+    won_recv,
+    p_send,
+    p_recv,
+):
+    ring = 2 * half
+    z = lax.axis_index("tok")
+    m = lax.axis_index("mdl")
+    gid = lax.axis_index("grp")
+    ahead = lax.rem(z + 1, ring)
+    behind = lax.rem(z + ring - 1, ring)
+    odd_a = lax.rem(gid // side, 2)
+    odd_b = lax.rem(gid, 2)
+    neighbours = ({"grp": gid + side * (1 - 2 * odd_a)}, {"grp": gid + 1 - 2 * odd_b})
+    own = 2 * odd_a + odd_b
+    quarters = (own, 3 - own)
+    partner = {"mdl": 1 - m}
+    span, wide_half = hid_ref.shape
+    block = span // 2
+    width = resid_ref.shape[1]
+    chip_cols = width // ring
+    kv_heads = keys.shape[0]
+    positions = keys.shape[1]
+    head_total, _, head_dim = qs.shape
+    per_group = head_total // kv_heads
+    rows = per_group * span
+    scale = 1.0 / math.sqrt(head_dim)
+
+    load = pltpu.make_async_copy(cache_hbm, raw, csem.at[0])
+    load.start()
+
+    barrier = pltpu.get_barrier_semaphore()
+    for who in ({"tok": ahead}, {"tok": behind}, *neighbours, partner):
+        pl.semaphore_signal(barrier, inc=1, device_id=who, device_id_type=MESH)
+
+    four = 2 * kv_heads
+    perm4 = permutation(four, 64 * four)
+    for q in range(4):
+        got = jnp.dot(perm4, wkv_ref[q], preferred_element_type=f32).astype(bf16)
+        for j in range(four):
+            kvbuf[0, q, :, pl.ds(j * head_dim, head_dim)] = got[j * 64 : (j + 1) * 64]
+    pl.semaphore_wait(barrier, 5)
+
+    hid_copy = pltpu.make_async_remote_copy(
+        src_ref=hid_ref,
+        dst_ref=hfull.at[m],
+        send_sem=h_send.at[0],
+        recv_sem=h_recv.at[0],
+        device_id=partner,
+        device_id_type=MESH,
     )
-    angle = positions.astype(jnp.float32)[:, None] * inverse[None, :]
-    cosine = jnp.cos(angle)[:, None, :]
-    sine_vals = jnp.sin(angle)[:, None, :]
-    front_half = key_rows[..., :half_dim]
-    back_half = key_rows[..., half_dim:]
-    return jnp.concatenate(
-        [front_half * cosine - back_half * sine_vals, back_half * cosine + front_half * sine_vals],
-        axis=-1,
+    hid_copy.start()
+
+    kinds = {
+        "kv": (kvbuf, kv_send, kv_recv, kvn_send, kvn_recv),
+        "wo": (wobuf, wo_send, wo_recv, won_send, won_recv),
+    }
+
+    def slot_of(step, flow):
+        return 1 if isinstance(step, int) and step == half else 2 * step + flow
+
+    def ring_copy(kind, src, step, flow, piece):
+        buf, send, recv, _, _ = kinds[kind]
+        q = quarters[piece]
+        return pltpu.make_async_remote_copy(
+            src_ref=src.at[q],
+            dst_ref=buf.at[slot_of(step, flow), q],
+            send_sem=send.at[step, flow, piece],
+            recv_sem=recv.at[step, flow, piece],
+            device_id={"tok": behind if flow == 0 else ahead},
+            device_id_type=MESH,
+        )
+
+    def side_copy(kind, slot, axis):
+        buf, _, _, send, recv = kinds[kind]
+        return pltpu.make_async_remote_copy(
+            src_ref=buf.at[slot, own],
+            dst_ref=buf.at[slot, own],
+            send_sem=send.at[slot, axis],
+            recv_sem=recv.at[slot, axis],
+            device_id=neighbours[axis],
+            device_id_type=MESH,
+        )
+
+    def arrive(kind, step):
+        buf = kinds[kind][0]
+        for piece in range(2):
+            for flow in range(2):
+                final = isinstance(step, int) and step == half
+                if final and flow != piece:
+                    continue
+                slot = slot_of(step, flow)
+                ring_copy(kind, buf.at[slot], step, flow, piece).wait_recv()
+                if not final:
+                    turn = isinstance(step, int) and step == half - 1
+                    if not turn or flow == piece:
+                        ring_copy(kind, buf.at[slot], step + 1, flow, piece).start()
+                if piece == 0:
+                    for axis in range(2):
+                        side_copy(kind, slot, axis).start()
+
+    def settle(kind, slot):
+        for axis in range(2):
+            side_copy(kind, slot, axis).wait_recv()
+
+    for piece in range(2):
+        for flow in range(2):
+            ring_copy("kv", kvbuf.at[0], 1, flow, piece).start()
+    for piece in range(2):
+        for flow in range(2):
+            ring_copy("wo", wo_ref, 1, flow, piece).start()
+
+    lane = lax.broadcasted_iota(jnp.int32, (16, block), 0)
+    route = jnp.zeros((16, block), f32)
+    for k in range(TOPK):
+        hit = (ids_ref[k : k + 1, :] == lane) | (ids_ref[k : k + 1, :] + EXPERTS == lane)
+        route = route + jnp.where(hit, gates_ref[k : k + 1, :], 0.0)
+    high = route.astype(bf16).astype(f32)
+    terms = jnp.where(lane < EXPERTS, high, route - high)
+    place = lax.broadcasted_iota(jnp.int32, (16, LANES), 0) == lax.broadcasted_iota(
+        jnp.int32, (16, LANES), 1
     )
-
-
-def score_rows(query_rows, key_rows, scale_factor):
-    return (
-        lax.dot_general(
-            query_rows, key_rows, (((1,), (1,)), ((), ())), preferred_element_type=jnp.float32
-        )
-        * scale_factor
+    tail = lax.dot_general(
+        terms.astype(bf16),
+        jnp.where(place, 1.0, 0.0).astype(bf16),
+        (((0,), (0,)), ((), ())),
+        preferred_element_type=f32,
     )
-
-
-def head_attention(query_rows, cache_keys, cache_values, length, new_keys, new_values, head_group):
-    row_count = query_rows.shape[0]
-    block_len = min(512, cache_keys.shape[0])
-    scale_factor = 1.0 / math.sqrt(query_rows.shape[1])
-    token_of_row = jnp.arange(row_count) // head_group
-    block_total = (length + block_len - 1) // block_len
-
-    def block_scores(block_idx):
-        row_offset = block_idx * block_len
-        block_keys = lax.dynamic_slice_in_dim(cache_keys, row_offset, block_len, 0)
-        allowed = row_offset + jnp.arange(block_len) < length
-        return (
-            jnp.where(
-                allowed[None, :], score_rows(query_rows, block_keys, scale_factor), mask_fill
-            ),
-            allowed,
-        )
-
-    new_allowed = jnp.arange(new_keys.shape[0])[None, :] <= token_of_row[:, None]
-    new_scores = jnp.where(new_allowed, score_rows(query_rows, new_keys, scale_factor), mask_fill)
-    first_max = jnp.max(new_scores, axis=1)
-    first_sum = jnp.sum(
-        jnp.where(new_allowed, jnp.exp(new_scores - first_max[:, None]), 0.0), axis=1
+    x_ref[:, pl.ds(width, LANES)] = tail.astype(bf16)
+
+    perm_q = permutation(head_total, 32 * head_total)
+    for b in range(span // 32):
+        got = jnp.dot(perm_q, q_ref[b], preferred_element_type=f32).astype(bf16)
+        for h in range(head_total):
+            qs[h, pl.ds(32 * b, 32), :] = got[32 * h : 32 * (h + 1)]
+
+    hfull[m] = hid_ref[...]
+    hid_copy.wait_recv()
+    square = jnp.zeros((span, LANES), f32)
+    for j in range(width // LANES):
+        v = hfull[j // (ring // 2 * chip_cols // LANES), :, pl.ds(j * LANES % wide_half, LANES)]
+        v = v.astype(f32)
+        square = square + v * v
+    inv = lax.rsqrt(jnp.sum(square, axis=1, keepdims=True) / width + eps_norm)
+    for c in range(ring):
+        v = hfull[c * chip_cols // wide_half, :, pl.ds(c * chip_cols % wide_half, chip_cols)]
+        gain = again_ref[:, pl.ds(c * chip_cols, chip_cols)].astype(f32)
+        normed[c] = (v.astype(f32) * inv * gain).astype(bf16)
+
+    def chip_of(slot):
+        if isinstance(slot, int) and slot < 2:
+            return lax.rem(z + slot * half, ring)
+        step, flow = slot // 2, lax.rem(slot, 2)
+        return lax.rem(z + ring + step * (1 - 2 * flow), ring)
+
+    def kv_use(slot):
+        weights = kvbuf[slot].reshape(chip_cols, four * head_dim)
+        kvacc[...] += jnp.dot(normed[chip_of(slot)], weights, preferred_element_type=f32)
+
+    kvacc[...] = jnp.zeros_like(kvacc)
+    kv_use(0)
+
+    load.wait()
+
+    def unpack(b, carry):
+        got = jnp.dot(
+            perm4,
+            raw[pl.ds(pl.multiple_of(b * 64 * four, 64 * four), 64 * four), :],
+            preferred_element_type=f32,
+        ).astype(bf16)
+        at = pl.ds(pl.multiple_of(b * 64, 64), 64)
+        for g in range(kv_heads):
+            keys[g, at, :] = got[(2 * g) * 64 : (2 * g + 1) * 64]
+            vals[g, at, :] = got[(2 * g + 1) * 64 : (2 * g + 2) * 64]
+        return carry
+
+    lax.fori_loop(0, positions // 64, unpack, 0)
+
+    length = len_ref[0]
+    smax[...] = jnp.full_like(smax, mask_fill)
+    ssum[...] = jnp.zeros_like(ssum)
+    sacc[...] = jnp.zeros_like(sacc)
+
+    def attend(g, key_rows, value_rows, allowed):
+        query_rows = qs[pl.ds(per_group * g, per_group)].reshape(rows, head_dim)
+        scores = lax.dot_general(
+            query_rows, key_rows, (((1,), (1,)), ((), ())), preferred_element_type=f32
+        )
+        scores = jnp.where(allowed, scores * scale, mask_fill)
+        old = smax[g][:, :1]
+        top = jnp.maximum(old, jnp.max(scores, axis=1, keepdims=True))
+        weights = jnp.where(allowed, jnp.exp(scores - top), 0.0)
+        fade = jnp.exp(old - top)
+        smax[g] = jnp.broadcast_to(top, (rows, LANES))
+        ssum[g] = ssum[g] * fade + jnp.sum(weights, axis=1, keepdims=True)
+        sacc[g] = sacc[g] * fade + jnp.dot(
+            weights.astype(bf16), value_rows, preferred_element_type=f32
+        )
+
+    key_blocks = positions // KEYS
+
+    def cached(i):
+        g = i // key_blocks
+        lo = lax.rem(i, key_blocks) * KEYS
+        if not isinstance(lo, int):
+            lo = pl.multiple_of(lo, KEYS)
+        col = lo + lax.broadcasted_iota(jnp.int32, (rows, KEYS), 1)
+        attend(g, keys[g, pl.ds(lo, KEYS), :], vals[g, pl.ds(lo, KEYS), :], col < length)
+
+    def kv_step(step):
+        arrive("kv", step)
+        cached(step - 1)
+
+    def kv_settled(step):
+        for flow in range(2):
+            settle("kv", slot_of(step, flow))
+            kv_use(slot_of(step, flow))
+
+    kv_step(1)
+
+    def pair(k):
+        kv_step(2 * k)
+        kv_settled(2 * k - 1)
+        arrive("wo", k)
+        kv_step(2 * k + 1)
+        kv_settled(2 * k)
+
+    def pairs(k, carry):
+        pair(k)
+        return carry
+
+    lax.fori_loop(1, half // 2 - 1, pairs, 0)
+    pair(half // 2 - 1)
+    arrive("kv", half)
+    kv_settled(half - 1)
+    cached(jnp.int32(half - 1))
+    arrive("wo", half // 2)
+    settle("kv", 1)
+    kv_use(1)
+
+    lanes = lax.broadcasted_iota(jnp.int32, (span, head_dim), 1)
+    place_of = lax.broadcasted_iota(jnp.int32, (span, head_dim), 0) + length
+    pair_of = lax.rem(lanes, head_dim // 2).astype(f32)
+    angle = place_of.astype(f32) * jnp.exp(pair_of * (-2.0 * math.log(rope_base) / head_dim))
+    cosine = jnp.cos(angle)
+    sine = jnp.where(lanes < head_dim // 2, -jnp.sin(angle), jnp.sin(angle))
+    token = lax.rem(lax.broadcasted_iota(jnp.int32, (rows, span), 0), span)
+    causal = lax.broadcasted_iota(jnp.int32, (rows, span), 1) <= token
+    for g in range(kv_heads):
+        k_cols = pl.ds(2 * g * head_dim, head_dim)
+        v_cols = pl.ds((2 * g + 1) * head_dim, head_dim)
+        key = kvacc[:, k_cols]
+        turned = pltpu.roll(key, head_dim // 2, 1)
+        fresh_ref[:, k_cols] = (key * cosine + turned * sine).astype(bf16)
+        fresh_ref[:, v_cols] = kvacc[:, v_cols].astype(bf16)
+        attend(g, fresh_ref[:, k_cols], fresh_ref[:, v_cols], causal)
+        done = (sacc[g] / ssum[g]).astype(bf16)
+        for h in range(per_group):
+            at = pl.ds((g * per_group + h) * head_dim, head_dim)
+            heads[:, at] = done[h * span : (h + 1) * span]
+
+    def wo_use(slot, buf):
+        weights = buf.reshape(4 * wo_ref.shape[1], chip_cols)
+        got = jnp.dot(heads[...], weights, preferred_element_type=f32)
+        for core in range(2):
+            part[core, slot] = got[core * block : (core + 1) * block]
+
+    def part_copy(g):
+        return pltpu.make_async_remote_copy(
+            src_ref=part.at[1 - m, pl.ds(2 * g, 2)],
+            dst_ref=part_in.at[pl.ds(2 * g, 2)],
+            send_sem=p_send.at[g],
+            recv_sem=p_recv.at[g],
+            device_id=partner,
+            device_id_type=MESH,
+        )
+
+    def wo_settled(step):
+        for flow in range(2):
+            slot = slot_of(step, flow)
+            settle("wo", slot)
+            wo_use(slot, wobuf[slot])
+        part_copy(step).start()
+
+    def assemble(slot):
+        c = chip_of(slot)
+        cols = pl.ds(pl.multiple_of(c * chip_cols, chip_cols), chip_cols)
+        in_half = pl.ds(
+            pl.multiple_of(lax.rem(c * chip_cols, wide_half), chip_cols), chip_cols
+        )
+        mine = hfull[c * chip_cols // wide_half, pl.ds(pl.multiple_of(m * block, block), block), in_half]
+        resid_ref[:, cols] = mine.astype(f32) + part[m, slot] + part_in[slot]
+
+    def gather_parts(step):
+        part_copy(step).wait_recv()
+        for flow in range(2):
+            assemble(slot_of(step, flow))
+
+    wo_use(0, wo_ref[...])
+
+    def late(s, carry):
+        arrive("wo", s)
+        first = 2 * (s - half // 2) - 1
+        wo_settled(first)
+        wo_settled(first + 1)
+        return carry
+
+    lax.fori_loop(half // 2 + 1, half - 1, late, 0)
+    arrive("wo", half - 1)
+    wo_settled(half - 3)
+
+    def early(step, carry):
+        gather_parts(step)
+        return carry
+
+    lax.fori_loop(1, half - 3, early, 0)
+    arrive("wo", half)
+    wo_settled(half - 2)
+    wo_settled(half - 1)
+    lax.fori_loop(half - 3, half, early, 0)
+    settle("wo", 1)
+    wo_use(1, wobuf[1])
+    part_copy(0).start()
+    part_copy(0).wait_recv()
+    assemble(0)
+    assemble(1)
+
+    square = jnp.zeros((block, LANES), f32)
+    for j in range(width // LANES):
+        v = resid_ref[:, pl.ds(j * LANES, LANES)]
+        square = square + v * v
+    inv = lax.rsqrt(jnp.sum(square, axis=1, keepdims=True) / width + eps_norm)
+    for c in range(ring):
+        cols = pl.ds(c * chip_cols, chip_cols)
+        gain = mgain_ref[:, cols].astype(f32)
+        x_ref[:, cols] = (resid_ref[:, cols] * inv * gain).astype(bf16)
+
+    hid_copy.wait_send()
+
+    def drain_ring(step, carry):
+        for kind in ("kv", "wo"):
+            for flow in range(2):
+                for piece in range(2):
+                    ring_copy(kind, kinds[kind][0].at[0], step, flow, piece).wait_send()
+        return carry
+
+    lax.fori_loop(1, half, drain_ring, 0)
+    for kind in ("kv", "wo"):
+        for flow in range(2):
+            ring_copy(kind, kinds[kind][0].at[0], half, flow, flow).wait_send()
+
+    def drain_sides(slot, carry):
+        for kind in ("kv", "wo"):
+            for axis in range(2):
+                side_copy(kind, slot, axis).wait_send()
+        return carry
+
+    lax.fori_loop(1, ring, drain_sides, 0)
+
+    def drain_parts(g, carry):
+        part_copy(g).wait_send()
+        return carry
+
+    lax.fori_loop(0, half, drain_parts, 0)
+
+
+def prelude(hidden, queries, cache, cache_lengths, wkv, wo, attn_gain, moe_gain, expert_ids, gates):
+    ring = lax.axis_size("tok")
+    half = ring // 2
+    side = math.isqrt(lax.axis_size("grp"))
+    span, wide_half = hidden.shape
+    block, width = span // 2, 2 * wide_half
+    heads, head_dim = queries.shape[1:]
+    positions, kv_heads = cache.shape[1:3]
+    four = 2 * kv_heads
+    chip_cols = width // ring
+    rows = heads // kv_heads * span
+    vmem = pl.BlockSpec(memory_space=pltpu.VMEM)
+    hbm = pl.BlockSpec(memory_space=pl.ANY)
+    smem = pl.BlockSpec(memory_space=pltpu.SMEM)
+    dma = pltpu.SemaphoreType.DMA
+    depth = heads * head_dim // 4
+    return pl.pallas_call(
+        functools.partial(prelude_kernel, half, side),
+        out_shape=(
+            jax.ShapeDtypeStruct((block, width + LANES), bf16),
+            jax.ShapeDtypeStruct((block, width), f32),
+            jax.ShapeDtypeStruct((span, four * head_dim), bf16),
+        ),
+        in_specs=[vmem, vmem, hbm, smem, vmem, vmem, vmem, vmem, vmem, vmem],
+        out_specs=(vmem, vmem, vmem),
+        scratch_shapes=[
+            pltpu.VMEM((2, span, wide_half), bf16),
+            pltpu.VMEM((ring, span, chip_cols), bf16),
+            pltpu.VMEM((ring, 4, chip_cols // 4, four * head_dim), bf16),
+            pltpu.VMEM((ring, 4, depth, chip_cols), bf16),
+            pltpu.VMEM((positions * four, head_dim), bf16),
+            pltpu.VMEM((kv_heads, positions, head_dim), bf16),
+            pltpu.VMEM((kv_heads, positions, head_dim), bf16),
+            pltpu.VMEM((heads, span, head_dim), bf16),
+            pltpu.VMEM((span, four * head_dim), f32),
+            pltpu.VMEM((kv_heads, rows, LANES), f32),
+            pltpu.VMEM((kv_heads, rows, LANES), f32),
+            pltpu.VMEM((kv_heads, rows, head_dim), f32),
+            pltpu.VMEM((span, heads * head_dim), bf16),
+            pltpu.VMEM((2, ring, block, chip_cols), f32),
+            pltpu.VMEM((ring, block, chip_cols), f32),
+            dma((1,)),
+            dma((1,)),
+            dma((1,)),
+            dma((half + 1, 2, 2)),
+            dma((half + 1, 2, 2)),
+            dma((ring, 2)),
+            dma((ring, 2)),
+            dma((half + 1, 2, 2)),
+            dma((half + 1, 2, 2)),
+            dma((ring, 2)),
+            dma((ring, 2)),
+            dma((half,)),
+            dma((half,)),
+        ],
+        compiler_params=pltpu.CompilerParams(
+            collective_id=0, has_side_effects=True, vmem_limit_bytes=56 * 1024 * 1024
+        ),
+        name="prelude",
+    )(
+        hidden,
+        queries.reshape(span // 32, 32 * heads, head_dim),
+        cache.reshape(positions * four, head_dim),
+        cache_lengths,
+        wkv.reshape(4, chip_cols // 4 * four, head_dim),
+        wo.reshape(4, depth, chip_cols),
+        attn_gain.reshape(1, width),
+        moe_gain.reshape(1, width),
+        expert_ids.T,
+        gates.T,
     )
 
-    def first_pass(block_idx, carry):
-        run_max, run_sum = carry
-        scores, allowed = block_scores(block_idx)
-        next_max = jnp.maximum(run_max, jnp.max(scores, axis=1))
-        weights = jnp.where(allowed[None, :], jnp.exp(scores - next_max[:, None]), 0.0)
-        return (next_max, run_sum * jnp.exp(run_max - next_max) + jnp.sum(weights, axis=1))
-
-    row_max, row_sum = lax.fori_loop(0, block_total, first_pass, (first_max, first_sum))
-    new_probs = (
-        jnp.where(new_allowed, jnp.exp(new_scores - row_max[:, None]), 0.0) / row_sum[:, None]
-    ).astype(jnp.bfloat16)
-    start_total = jnp.dot(new_probs, new_values, preferred_element_type=jnp.float32)
-
-    def second_pass(block_idx, total):
-        scores, allowed = block_scores(block_idx)
-        probs = (
-            jnp.where(allowed[None, :], jnp.exp(scores - row_max[:, None]), 0.0) / row_sum[:, None]
-        ).astype(jnp.bfloat16)
-        block_values = lax.dynamic_slice_in_dim(cache_values, block_idx * block_len, block_len, 0)
-        return total + jnp.dot(probs, block_values, preferred_element_type=jnp.float32)
-
-    total = lax.fori_loop(0, block_total, second_pass, start_total)
-    return total.astype(jnp.bfloat16)
-
-
-LANES = 128
+
 GT = 256
 DT = 512
 
@@ -463,60 +844,11 @@
     expert_ids,
     gates,
 ):
-    full_rows = collect(hidden, "mdl", 1)
-    span_len = full_rows.shape[0]
-    normalized_input = rms_scale(full_rows, attn_gain).astype(jnp.bfloat16)
-    kv_heads = wkv.shape[1]
-    head_dim = wkv.shape[3]
-    weight_piece = lax.all_gather(wkv, "tok", axis=0, tiled=True)
-    key_value_projection = jnp.dot(
-        normalized_input,
-        weight_piece.reshape(weight_piece.shape[0], -1),
-        preferred_element_type=jnp.float32,
-    ).reshape(span_len, kv_heads, 2, head_dim)
-    length = cache_lengths[0]
-    positions = length + jnp.arange(span_len, dtype=jnp.int32)
-    fresh_key_value = jnp.stack(
-        [rotate(key_value_projection[:, :, 0], positions), key_value_projection[:, :, 1]], axis=2
-    ).astype(jnp.bfloat16)
-    head_group = queries.shape[1] // kv_heads
-    outputs = []
-    for head_index in range(kv_heads):
-        query_rows = queries[:, head_index * head_group : (head_index + 1) * head_group].reshape(
-            span_len * head_group, head_dim
-        )
-        attended = head_attention(
-            query_rows,
-            cache[0, :, head_index, 0],
-            cache[0, :, head_index, 1],
-            length,
-            fresh_key_value[:, head_index, 0],
-            fresh_key_value[:, head_index, 1],
-            head_group,
-        )
-        outputs.append(attended.reshape(span_len, head_group * head_dim))
-    heads_out = jnp.concatenate(outputs, axis=1)
-    weight_piece = lax.all_gather(wo, "tok", axis=2, tiled=True)
-    attn_out = jnp.dot(
-        heads_out,
-        weight_piece.reshape(-1, weight_piece.shape[2]),
-        preferred_element_type=jnp.float32,
+    x_wide, resid, fresh = prelude(
+        hidden, queries, cache, cache_lengths, wkv, wo, attn_gain, moe_gain, expert_ids, gates
     )
-    core_rows = span_len // lax.axis_size("mdl")
-    core_start = lax.axis_index("mdl") * core_rows
-    attn_rows = sent_and_summed(attn_out, "mdl", 0)
-    resid = (
-        lax.dynamic_slice_in_dim(full_rows, core_start, core_rows, 0).astype(jnp.float32)
-        + attn_rows
-    )
-    moe_in = rms_scale(resid, moe_gain).astype(jnp.bfloat16)
-    matches = expert_ids[:, :, None] == jnp.arange(EXPERTS)[None, None, :]
-    route = jnp.sum(jnp.where(matches, gates[:, :, None], 0.0), axis=1)
-    high = route.astype(bf16)
-    low = (route - high.astype(f32)).astype(bf16)
-    pad = jnp.zeros((core_rows, LANES - 2 * EXPERTS), bf16)
-    x_wide = jnp.concatenate([moe_in, high, low, pad], axis=1)
     mixed = expert_layer(x_wide, resid, w_gate[0], w_up[0], w_down[0])
+    fresh_key_value = fresh.reshape(fresh.shape[0], *wkv.shape[1:])
     return (mixed, fresh_key_value)
 
 

time: 349 us -> 217 us (0.62)
  waiting for transfers between devices: 149 us -> 0 us
  Pallas kernels: 113 us -> 209 us
  local copies, waits for them, and re-layouts: 25.8 us -> 5.78 us
  blocking collectives: 14.5 us -> 0 us
  between operations: 15 us -> 1.29 us
  starting transfers between devices: 13.5 us -> 0 us
  matrix products: 11.8 us -> 0 us
  other arithmetic: 5 us -> 0 us
    all_gather x2 -> x0, waiting for transfers between devices: 147 us -> none  [the longest x1 99.7 us: shards(): weight_piece = lax.all_gather(wo, 'tok', axis=2, tiled=True)]
    pallas_call x0 -> x1, Pallas kernels: none -> 97 us  [prelude(): pl.pallas_call(functools.partial(prelude_kernel, half, side), out_shape=(...]
    all_to_all x1 -> x0, blocking collectives: 14.5 us -> none  [sent_and_summed(): lax.all_to_all(tiles, axis, split_axis=0, concat_axis=0, tiled=True)]
    all_to_all x1 -> x0, starting transfers between devices: 13.4 us -> none  [sent_to_all(): return lax.all_to_all(copies, axis, split_axis=0, concat_axis=0, tiled=True)]
    dot_general x10 -> x0, matrix products: 11.8 us -> none  [the longest x1 4.97 us: shards(): jnp.dot(heads_out, weight_piece.reshape(-1, weight_piece.shape[2]), prefe...]
    reshape x2 -> x3, local copies, waits for them, and re-layouts: 12 us -> 4.11 us  [the longest x1 1.49 us: shards(): fresh_key_value = fresh.reshape(fresh.shape[0], *wkv.shape[1:])]
  transfers between devices with their start and end apart: 3 -> 0, of which waited for: 2 -> 0; matrix products, arithmetic and copies ran while one was open for 10% -> 0% of each run, Pallas kernels for 0% -> 0%
where the time goes in v2:
time: 217 us; the launch traced here: 216 us
  Pallas kernels  209 us (96%)
  local copies, waits for them, and re-layouts  5.78 us (3%)
    pallas_call x1, Pallas kernels, expert_layer(): pl.pallas_call(functools.partial(expert_kernel, half), out_shape=jax.Shap...  112 us
    pallas_call x1, Pallas kernels, prelude(): pl.pallas_call(functools.partial(prelude_kernel, half, side), out_shape=(...  97 us

profile of v2, /device:TPU:69, one launch (start us, length us, event | category | flops | bytes accessed | tf_op | source)
XLA Modules:
  0.0 216.4 jit_solution(13537889980710493119)
XLA Ops:
  1.3 1.3 reshape.29.again_ref
  2.6 1.3 reshape.30.mgain_ref
  3.9 97.0 %prelude.1 = (bf16[32,4224]{1,0:T(8,128)(2,1)}, f32[32,4096]{1,0:T(8,128)}, bf16[64,512]{1,0:T(8,128)(2,1)}) custom-call(bf16[64,2048]{1,0:T(8,128)(2,1)} %hid_ref.1, bf16[2,256,128]{2,1,0:T(8,128)(2,1)} %bitcast.15, bf16[8192,128]{1,0:T(8,128)(2,1)} %bitcast.12, s32[1]{0:T(128)S(6)} %copy.16.len_ref, bf16[4,256,128]{2,1,0:T(8,128)(2,1)} %bitcast.14, ...), custom_call_target="tpu_custom_call" | custom-call | tf_op jit(solution)/shard_map/prelude/pallas_call | solution.py:456
  100.9 112.4 %expert_layer.1 = bf16[32,4096]{1,0:T(8,128)(2,1)} custom-call(bf16[32,4224]{1,0:T(8,128)(2,1)} %get-tuple-element.5.x_ref, f32[32,4096]{1,0:T(8,128)} %get-tuple-element.6.resid_ref, bf16[4096,896]{1,0:T(8,128)(2,1)} %bitcast.9, bf16[4096,896]{1,0:T(8,128)(2,1)} %bitcast.10, bf16[896,4096]{1,0:T(8,128)(2,1)} %bitcast.11), custom_call_target="tpu_custom_call" | custom-call | tf_op jit(solution)/shard_map/expert_layer/pallas_call | solution.py:800
  213.3 1.5 reshape.31
  214.7 1.7 copy.17

commit v3 on v2

--- a/solution.py
+++ b/solution.py
@@ -155,9 +155,9 @@
             device_id_type=MESH,
         )
 
-    def arrive(kind, step):
+    def arrive(kind, step, pieces=(0, 1)):
         buf = kinds[kind][0]
-        for piece in range(2):
+        for piece in pieces:
             for flow in range(2):
                 final = isinstance(step, int) and step == half
                 if final and flow != piece:
@@ -207,6 +207,11 @@
         for h in range(head_total):
             qs[h, pl.ds(32 * b, 32), :] = got[32 * h : 32 * (h + 1)]
 
+    def gain_of(ref, c):
+        each = chip_cols // LANES
+        gains = [ref[c * each + j : c * each + j + 1, :].astype(f32) for j in range(each)]
+        return jnp.concatenate(gains, axis=1)
+
     hfull[m] = hid_ref[...]
     hid_copy.wait_recv()
     square = jnp.zeros((span, LANES), f32)
@@ -217,7 +222,7 @@
     inv = lax.rsqrt(jnp.sum(square, axis=1, keepdims=True) / width + eps_norm)
     for c in range(ring):
         v = hfull[c * chip_cols // wide_half, :, pl.ds(c * chip_cols % wide_half, chip_cols)]
-        gain = again_ref[:, pl.ds(c * chip_cols, chip_cols)].astype(f32)
+        gain = gain_of(again_ref, c)
         normed[c] = (v.astype(f32) * inv * gain).astype(bf16)
 
     def chip_of(slot):
@@ -290,12 +295,14 @@
             kv_use(slot_of(step, flow))
 
     kv_step(1)
+    arrive("wo", 1, (0,))
 
     def pair(k):
         kv_step(2 * k)
+        arrive("wo", k, (1,))
         kv_settled(2 * k - 1)
-        arrive("wo", k)
         kv_step(2 * k + 1)
+        arrive("wo", k + 1, (0,))
         kv_settled(2 * k)
 
     def pairs(k, carry):
@@ -305,9 +312,9 @@
     lax.fori_loop(1, half // 2 - 1, pairs, 0)
     pair(half // 2 - 1)
     arrive("kv", half)
+    arrive("wo", half // 2, (1,))
     kv_settled(half - 1)
     cached(jnp.int32(half - 1))
-    arrive("wo", half // 2)
     settle("kv", 1)
     kv_use(1)
 
@@ -405,7 +412,7 @@
     inv = lax.rsqrt(jnp.sum(square, axis=1, keepdims=True) / width + eps_norm)
     for c in range(ring):
         cols = pl.ds(c * chip_cols, chip_cols)
-        gain = mgain_ref[:, cols].astype(f32)
+        gain = gain_of(mgain_ref, c)
         x_ref[:, cols] = (resid_ref[:, cols] * inv * gain).astype(bf16)
 
     hid_copy.wait_send()
@@ -449,7 +456,7 @@
     chip_cols = width // ring
     rows = heads // kv_heads * span
     vmem = pl.BlockSpec(memory_space=pltpu.VMEM)
-    hbm = pl.BlockSpec(memory_space=pl.ANY)
+    hbm = pl.BlockSpec(memory_space=pltpu.HBM)
     smem = pl.BlockSpec(memory_space=pltpu.SMEM)
     dma = pltpu.SemaphoreType.DMA
     depth = heads * head_dim // 4
@@ -493,7 +500,7 @@
             dma((half,)),
         ],
         compiler_params=pltpu.CompilerParams(
-            collective_id=0, has_side_effects=True, vmem_limit_bytes=56 * 1024 * 1024
+            collective_id=0, has_side_effects=True, vmem_limit_bytes=67043328
         ),
         name="prelude",
     )(
@@ -503,8 +510,8 @@
         cache_lengths,
         wkv.reshape(4, chip_cols // 4 * four, head_dim),
         wo.reshape(4, depth, chip_cols),
-        attn_gain.reshape(1, width),
-        moe_gain.reshape(1, width),
+        attn_gain.reshape(width // LANES, LANES),
+        moe_gain.reshape(width // LANES, LANES),
         expert_ids.T,
         gates.T,
     )
@@ -512,6 +519,7 @@
 
 GT = 256
 DT = 512
+PIECES = 2
 
 
 def expert_kernel(
@@ -550,10 +558,10 @@
     expert = z // (ring // EXPERTS)
     block, width = resid_ref.shape
     ffs = wg_hbm.shape[1]
-    wide = x_ref.shape[1]
-    cut = width // 2
-    spans = ((0, cut), (cut, wide - cut))
-    ospans = ((0, cut), (cut, width - cut))
+    cut = width // PIECES
+    spans = [(i * cut, cut) for i in range(PIECES)]
+    wide_spans = spans[:-1] + [(width - cut, cut + LANES)]
+    side_of = [i * 2 // PIECES for i in range(PIECES)]
 
     loads = (
         pltpu.make_async_copy(wg_hbm, wgu.at[:, pl.ds(0, ffs)], wsem.at[0]),
@@ -567,10 +575,10 @@
     pl.semaphore_wait(barrier, 3)
 
     def ring_copy(src, dst_slot, flow, piece, step):
-        lo, size = spans[piece]
+        cols = pl.ds(*wide_spans[piece])
         return pltpu.make_async_remote_copy(
-            src_ref=src.at[:, pl.ds(lo, size)],
-            dst_ref=xs.at[dst_slot, 0, :, pl.ds(lo, size)],
+            src_ref=src.at[:, cols],
+            dst_ref=xs.at[dst_slot, 0, :, cols],
             send_sem=ag_send.at[step, flow, piece],
             recv_sem=ag_recv.at[step, flow, piece],
             device_id={"tok": behind if flow == 0 else ahead},
@@ -578,25 +586,22 @@
         )
 
     def partner_copy(src, slot, piece):
-        lo, size = spans[piece]
+        cols = pl.ds(*wide_spans[piece])
         return pltpu.make_async_remote_copy(
-            src_ref=src.at[:, pl.ds(lo, size)],
-            dst_ref=xs.at[slot, 1, :, pl.ds(lo, size)],
+            src_ref=src.at[:, cols],
+            dst_ref=xs.at[slot, 1, :, cols],
             send_sem=x_send.at[slot, piece],
             recv_sem=x_recv.at[slot, piece],
             device_id=partner,
             device_id_type=MESH,
         )
 
-    def first_slot(flow, piece):
-        return 2 + flow if half > 1 else 1
-
-    for piece in range(2):
+    for piece in range(PIECES):
         for flow in range(2):
             ring_copy(x_ref, 2 + flow, flow, piece, 1).start()
     for load in loads:
         load.start()
-    for piece in range(2):
+    for piece in range(PIECES):
         partner_copy(x_ref, 0, piece).start()
     xs[0, 0] = x_ref[...]
 
@@ -637,19 +642,20 @@
     gtiles = 2 * ffs // GT
     dtiles = width // DT
 
-    def give(g):
+    def give(g, side):
+        cols = pl.ds(side * (width // 2), width // 2)
         return pltpu.make_async_remote_copy(
-            src_ref=pout.at[pl.ds(2 * g, 2)],
-            dst_ref=pin.at[pl.ds(2 * g, 2)],
-            send_sem=p_send.at[g],
-            recv_sem=p_recv.at[g],
+            src_ref=pout.at[pl.ds(2 * g, 2), :, cols],
+            dst_ref=pin.at[pl.ds(2 * g, 2), :, cols],
+            send_sem=p_send.at[g, side],
+            recv_sem=p_recv.at[g, side],
             device_id=partner,
             device_id_type=MESH,
         )
 
     def await_partner(g):
         for slot in range(2):
-            for piece in range(2):
+            for piece in range(PIECES):
                 partner_copy(x_ref, 2 * g + slot, piece).wait_recv()
 
     def arrive(s, flow, piece, onward):
@@ -658,58 +664,68 @@
             ring_copy(xs.at[2 * s + flow, 0], onward, flow, piece, s + 1).start()
         partner_copy(xs.at[2 * s + flow, 0], 2 * s + flow, piece).start()
 
-    def first_part(g):
-        await_partner(g)
-        gate_up(g, 0, gtiles)
-
-    def second_part(g):
-        activate()
-        down(g, 0, dtiles)
-        give(g).start()
-
-    for flow in range(2):
-        arrive(1, flow, 0, 4 + flow)
-    for load in loads:
-        load.wait()
-    for flow in range(2):
-        arrive(1, flow, 1, 4 + flow)
+    def parts(g):
+        def first():
+            await_partner(g)
+            gate_up(g, 0, gtiles // 2)
+
+        def second():
+            gate_up(g, gtiles // 2, gtiles)
+
+        def third():
+            activate()
+            down(g, 0, dtiles // 2)
+            give(g, 0).start()
+
+        def fourth():
+            down(g, dtiles // 2, dtiles)
+            give(g, 1).start()
+
+        return first, second, third, fourth
+
+    def spread(todo, piece):
+        for i, part in enumerate(todo):
+            if i * PIECES // 4 == piece:
+                part()
+
+    for piece in range(PIECES):
+        for flow in range(2):
+            arrive(1, flow, piece, 4 + flow)
+        if piece == 0:
+            for load in loads:
+                load.wait()
 
     def body(s, carry):
-        for flow in range(2):
-            arrive(s, flow, 0, 2 * (s + 1) + flow)
-        first_part(s - 1)
-        for flow in range(2):
-            arrive(s, flow, 1, 2 * (s + 1) + flow)
-        second_part(s - 1)
+        todo = parts(s - 1)
+        for piece in range(PIECES):
+            for flow in range(2):
+                arrive(s, flow, piece, 2 * (s + 1) + flow)
+            spread(todo, piece)
         return carry
 
     lax.fori_loop(2, half - 1, body, 0)
 
     last = half - 1
-    arrive(last, 0, 0, 1)
-    arrive(last, 1, 0, None)
-    first_part(last - 1)
-    arrive(last, 0, 1, None)
-    arrive(last, 1, 1, 1)
-    second_part(last - 1)
-
-    await_partner(last)
-    gate_up(last, 0, gtiles)
-    for flow in range(2):
-        ring_copy(x_ref, 1, flow, flow, half).wait_recv()
-        partner_copy(xs.at[1, 0], 1, flow).start()
-    second_part(last)
-    await_partner(0)
-    gate_up(0, 0, gtiles)
-    activate()
-    down(0, 0, dtiles)
-    give(0).start()
+    todo = parts(last - 1)
+    for piece in range(PIECES):
+        for flow in range(2):
+            arrive(last, flow, piece, 1 if flow == side_of[piece] else None)
+        spread(todo, piece)
+
+    todo = parts(last)
+    order = [i // 2 + (i % 2) * (PIECES // 2) for i in range(PIECES)]
+    for i, piece in enumerate(order):
+        ring_copy(x_ref, 1, side_of[piece], piece, half).wait_recv()
+        partner_copy(xs.at[1, 0], 1, piece).start()
+        spread(todo, i)
+    for part in parts(0):
+        part()
 
     def sum_copy(slot, flow, piece, step):
-        lo, size = ospans[piece]
+        cols = pl.ds(*spans[piece])
         return pltpu.make_async_remote_copy(
-            src_ref=mine.at[slot, :, pl.ds(lo, size)],
-            dst_ref=rsin.at[flow, step, :, pl.ds(lo, size)],
+            src_ref=mine.at[slot, :, cols],
+            dst_ref=rsin.at[flow, step, :, cols],
             send_sem=rs_send.at[step, flow, piece],
             recv_sem=rs_recv.at[step, flow, piece],
             device_id={"tok": ahead if flow == 0 else behind},
@@ -717,8 +733,7 @@
         )
 
     def add_and_send(slot, flow, piece, step, incoming):
-        lo, size = ospans[piece]
-        cols = pl.ds(lo, size)
+        cols = pl.ds(*spans[piece])
         total = mine[slot, :, cols].astype(f32) + pin[slot, :, cols].astype(f32)
         if incoming:
             sum_copy(slot, flow, piece, step - 1).wait_recv()
@@ -726,28 +741,31 @@
         mine[slot, :, cols] = total.astype(bf16)
         sum_copy(slot, flow, piece, step).start()
 
-    give(0).wait_recv()
     for flow in range(2):
-        add_and_send(1, flow, flow, 0, False)
-    give(last).wait_recv()
+        give(0, flow).wait_recv()
+        for piece in range(PIECES):
+            if side_of[piece] == flow:
+                add_and_send(1, flow, piece, 0, False)
     for flow in range(2):
-        add_and_send(2 * last + flow, flow, 1 - flow, 1, False)
-    for flow in range(2):
-        add_and_send(2 * last + flow, flow, flow, 1, True)
+        give(last, flow).wait_recv()
+    for incoming in (False, True):
+        for piece in range(PIECES):
+            flow = side_of[piece] if incoming else 1 - side_of[piece]
+            add_and_send(2 * last + flow, flow, piece, 1, incoming)
 
     def fold(step, carry):
         s = half - step
-        give(s).wait_recv()
-        for piece in range(2):
+        for side in range(2):
+            give(s, side).wait_recv()
+        for piece in range(PIECES):
             for flow in range(2):
                 add_and_send(2 * s + flow, flow, piece, step, True)
         return carry
 
     lax.fori_loop(2, half, fold, 0)
 
-    for piece in range(2):
-        lo, size = ospans[piece]
-        cols = pl.ds(lo, size)
+    for piece in range(PIECES):
+        cols = pl.ds(*spans[piece])
         total = resid_ref[:, cols] + mine[0, :, cols].astype(f32) + pin[0, :, cols].astype(f32)
         for flow in range(2):
             sum_copy(0, flow, piece, half - 1).wait_recv()
@@ -756,35 +774,36 @@
 
     def drain_ring(s, carry):
         for flow in range(2):
-            for piece in range(2):
+            for piece in range(PIECES):
                 ring_copy(x_ref, 1, flow, piece, s).wait_send()
         return carry
 
     lax.fori_loop(1, half, drain_ring, 0)
-    for flow in range(2):
-        ring_copy(x_ref, 1, flow, flow, half).wait_send()
+    for piece in range(PIECES):
+        ring_copy(x_ref, 1, side_of[piece], piece, half).wait_send()
 
     def drain_slots(slot, carry):
-        for piece in range(2):
+        for piece in range(PIECES):
             partner_copy(x_ref, slot, piece).wait_send()
         return carry
 
     lax.fori_loop(0, ring, drain_slots, 0)
 
     def drain_groups(g, carry):
-        give(g).wait_send()
+        for side in range(2):
+            give(g, side).wait_send()
         return carry
 
     lax.fori_loop(0, half, drain_groups, 0)
 
     def drain_sums(step, carry):
         for flow in range(2):
-            for piece in range(2):
+            for piece in range(PIECES):
                 sum_copy(0, flow, piece, step).wait_send()
         return carry
 
-    for flow in range(2):
-        sum_copy(0, flow, flow, 0).wait_send()
+    for piece in range(PIECES):
+        sum_copy(0, side_of[piece], piece, 0).wait_send()
     lax.fori_loop(1, half, drain_sums, 0)
 
 
@@ -795,7 +814,7 @@
     ffs = w_gate.shape[1]
     wide = x_wide.shape[1]
     vmem = pl.BlockSpec(memory_space=pltpu.VMEM)
-    hbm = pl.BlockSpec(memory_space=pl.ANY)
+    hbm = pl.BlockSpec(memory_space=pltpu.HBM)
     dma = pltpu.SemaphoreType.DMA
     return pl.pallas_call(
         functools.partial(expert_kernel, half),
@@ -813,14 +832,14 @@
             pltpu.VMEM((ring, block, width), bf16),
             pltpu.VMEM((2, half, block, width), bf16),
             dma((3,)),
-            dma((half + 1, 2, 2)),
-            dma((half + 1, 2, 2)),
-            dma((ring, 2)),
-            dma((ring, 2)),
-            dma((half,)),
-            dma((half,)),
-            dma((half, 2, 2)),
-            dma((half, 2, 2)),
+            dma((half + 1, 2, PIECES)),
+            dma((half + 1, 2, PIECES)),
+            dma((ring, PIECES)),
+            dma((ring, PIECES)),
+            dma((half, 2)),
+            dma((half, 2)),
+            dma((half, 2, PIECES)),
+            dma((half, 2, PIECES)),
         ],
         compiler_params=pltpu.CompilerParams(
             collective_id=1, has_side_effects=True, vmem_limit_bytes=67043328

time: 217 us -> 213 us (0.982)
  local copies, waits for them, and re-layouts: 5.78 us -> 3.16 us
    reshape x2 -> x0, local copies, waits for them, and re-layouts: 2.62 us -> none  [the longest x1 1.31 us: prelude(): attn_gain.reshape(1, width)]
where the time goes in v3:
time: 213 us
  Pallas kernels  209 us (98%)
  local copies, waits for them, and re-layouts  3.16 us (1%)
    pallas_call x1, Pallas kernels, expert_layer(): pl.pallas_call(functools.partial(expert_kernel, half), out_shape=jax.Shap...  112 us
    pallas_call x1, Pallas kernels, prelude(): pl.pallas_call(functools.partial(prelude_kernel, half, side), out_shape=(...  97 us

profile of v3, /device:TPU:69, one launch (start us, length us, event | category | flops | bytes accessed | tf_op | source)
XLA Modules:
  0.0 213.2 jit_solution(8748378209415416833)
XLA Ops:
  1.3 97.0 %prelude.1 = (bf16[32,4224]{1,0:T(8,128)(2,1)}, f32[32,4096]{1,0:T(8,128)}, bf16[64,512]{1,0:T(8,128)(2,1)}) custom-call(bf16[64,2048]{1,0:T(8,128)(2,1)} %hid_ref.1, bf16[2,256,128]{2,1,0:T(8,128)(2,1)} %bitcast.17, bf16[8192,128]{1,0:T(8,128)(2,1)} %bitcast.14, s32[1]{0:T(128)S(6)} %copy.16.len_ref, bf16[4,256,128]{2,1,0:T(8,128)(2,1)} %bitcast.16, ...), custom_call_target="tpu_custom_call" | custom-call | tf_op jit(solution)/shard_map/prelude/pallas_call | solution.py:463
  98.3 111.7 %expert_layer.1 = bf16[32,4096]{1,0:T(8,128)(2,1)} custom-call(bf16[32,4224]{1,0:T(8,128)(2,1)} %get-tuple-element.5.x_ref, f32[32,4096]{1,0:T(8,128)} %get-tuple-element.6.resid_ref, bf16[4096,896]{1,0:T(8,128)(2,1)} %bitcast.11, bf16[4096,896]{1,0:T(8,128)(2,1)} %bitcast.12, bf16[896,4096]{1,0:T(8,128)(2,1)} %bitcast.13), custom_call_target="tpu_custom_call" | custom-call | tf_op jit(solution)/shard_map/expert_layer/pallas_call | solution.py:819
  210.0 1.5 reshape.31
  211.5 1.7 copy.17

commit v4 on v3

--- a/solution.py
+++ b/solution.py
@@ -517,8 +517,6 @@
     )
 
 
-GT = 256
-DT = 512
 PIECES = 2
 
 
@@ -605,14 +603,9 @@
         partner_copy(x_ref, 0, piece).start()
     xs[0, 0] = x_ref[...]
 
-    def gate_up(g, lo, hi):
-        def tile(n, carry):
-            cols = pl.ds(pl.multiple_of(n * GT, GT), GT)
-            rows = xs[pl.ds(2 * g, 2), :, :, pl.ds(0, width)].reshape(4 * block, width)
-            gu[:, cols] = jnp.dot(rows, wgu[:, cols], preferred_element_type=f32)
-            return carry
-
-        lax.fori_loop(lo, hi, tile, 0)
+    def gate_up(g):
+        rows = xs[pl.ds(2 * g, 2), :, :, pl.ds(0, width)].reshape(4 * block, width)
+        gu[...] = jnp.dot(rows, wgu[...], preferred_element_type=f32)
 
     def activate():
         gate = gu[:, pl.ds(0, ffs)]
@@ -625,22 +618,14 @@
         pick = (lane == expert) | (lane == expert + EXPERTS)
         return jnp.sum(jnp.where(pick, tail.astype(f32), 0.0), axis=1, keepdims=True)
 
-    def down(g, lo, hi):
+    def down(g, side):
         weight = weight_of(g)
-
-        def tile(n, carry):
-            cols = pl.ds(pl.multiple_of(n * DT, DT), DT)
-            got = jnp.dot(hid[...], wd[:, cols], preferred_element_type=f32) * weight
-            got = got.astype(bf16)
-            for slot in range(2):
-                mine[2 * g + slot, :, cols] = got[2 * slot * block : (2 * slot + 1) * block]
-                pout[2 * g + slot, :, cols] = got[(2 * slot + 1) * block : (2 * slot + 2) * block]
-            return carry
-
-        lax.fori_loop(lo, hi, tile, 0)
-
-    gtiles = 2 * ffs // GT
-    dtiles = width // DT
+        cols = pl.ds(side * (width // 2), width // 2)
+        got = jnp.dot(hid[...], wd[:, cols], preferred_element_type=f32) * weight
+        got = got.astype(bf16)
+        for slot in range(2):
+            mine[2 * g + slot, :, cols] = got[2 * slot * block : (2 * slot + 1) * block]
+            pout[2 * g + slot, :, cols] = got[(2 * slot + 1) * block : (2 * slot + 2) * block]
 
     def give(g, side):
         cols = pl.ds(side * (width // 2), width // 2)
@@ -664,30 +649,6 @@
             ring_copy(xs.at[2 * s + flow, 0], onward, flow, piece, s + 1).start()
         partner_copy(xs.at[2 * s + flow, 0], 2 * s + flow, piece).start()
 
-    def parts(g):
-        def first():
-            await_partner(g)
-            gate_up(g, 0, gtiles // 2)
-
-        def second():
-            gate_up(g, gtiles // 2, gtiles)
-
-        def third():
-            activate()
-            down(g, 0, dtiles // 2)
-            give(g, 0).start()
-
-        def fourth():
-            down(g, dtiles // 2, dtiles)
-            give(g, 1).start()
-
-        return first, second, third, fourth
-
-    def spread(todo, piece):
-        for i, part in enumerate(todo):
-            if i * PIECES // 4 == piece:
-                part()
-
     for piece in range(PIECES):
         for flow in range(2):
             arrive(1, flow, piece, 4 + flow)
@@ -695,31 +656,39 @@
             for load in loads:
                 load.wait()
 
-    def body(s, carry):
-        todo = parts(s - 1)
-        for piece in range(PIECES):
+    last = half - 1
+
+    def events(s, piece):
+        @pl.when(s < last)
+        def _():
             for flow in range(2):
                 arrive(s, flow, piece, 2 * (s + 1) + flow)
-            spread(todo, piece)
-        return carry
-
-    lax.fori_loop(2, half - 1, body, 0)
-
-    last = half - 1
-    todo = parts(last - 1)
-    for piece in range(PIECES):
-        for flow in range(2):
-            arrive(last, flow, piece, 1 if flow == side_of[piece] else None)
-        spread(todo, piece)
-
-    todo = parts(last)
-    order = [i // 2 + (i % 2) * (PIECES // 2) for i in range(PIECES)]
-    for i, piece in enumerate(order):
-        ring_copy(x_ref, 1, side_of[piece], piece, half).wait_recv()
-        partner_copy(xs.at[1, 0], 1, piece).start()
-        spread(todo, i)
-    for part in parts(0):
-        part()
+
+        @pl.when(s == last)
+        def _():
+            for flow in range(2):
+                arrive(last, flow, piece, 1 if flow == side_of[piece] else None)
+
+        @pl.when(s == half)
+        def _():
+            ring_copy(x_ref, 1, side_of[piece], piece, half).wait_recv()
+            partner_copy(xs.at[1, 0], 1, piece).start()
+
+    def body(s, carry):
+        g = lax.rem(s - 1, half)
+        for piece in range(PIECES // 2):
+            events(s, piece)
+        await_partner(g)
+        gate_up(g)
+        for piece in range(PIECES // 2, PIECES):
+            events(s, piece)
+        activate()
+        for side in range(2):
+            down(g, side)
+            give(g, side).start()
+        return carry
+
+    lax.fori_loop(2, half + 2, body, 0)
 
     def sum_copy(slot, flow, piece, step):
         cols = pl.ds(*spans[piece])

time: 213 us -> 208 us (0.977)
  Pallas kernels: 209 us -> 203 us
    pallas_call x1, Pallas kernels: 112 us -> 106 us  [expert_layer(): pl.pallas_call(functools.partial(expert_kernel, half), out_shape=jax.Shap...]
where the time goes in v4:
time: 208 us; the launch traced here: 207 us
  Pallas kernels  203 us (98%)
  local copies, waits for them, and re-layouts  3.16 us (2%)
    pallas_call x1, Pallas kernels, expert_layer(): pl.pallas_call(functools.partial(expert_kernel, half), out_shape=jax.Shap...  106 us
    pallas_call x1, Pallas kernels, prelude(): pl.pallas_call(functools.partial(prelude_kernel, half, side), out_shape=(...  97 us

profile of v4, /device:TPU:69, one launch (start us, length us, event | category | flops | bytes accessed | tf_op | source)
XLA Modules:
  0.0 207.5 jit_solution(10572008136693059030)
XLA Ops:
  1.3 97.0 %prelude.1 = (bf16[32,4224]{1,0:T(8,128)(2,1)}, f32[32,4096]{1,0:T(8,128)}, bf16[64,512]{1,0:T(8,128)(2,1)}) custom-call(bf16[64,2048]{1,0:T(8,128)(2,1)} %hid_ref.1, bf16[2,256,128]{2,1,0:T(8,128)(2,1)} %bitcast.17, bf16[8192,128]{1,0:T(8,128)(2,1)} %bitcast.14, s32[1]{0:T(128)S(6)} %copy.16.len_ref, bf16[4,256,128]{2,1,0:T(8,128)(2,1)} %bitcast.16, ...), custom_call_target="tpu_custom_call" | custom-call | tf_op jit(solution)/shard_map/prelude/pallas_call | solution.py:463
  98.3 106.0 %expert_layer.1 = bf16[32,4096]{1,0:T(8,128)(2,1)} custom-call(bf16[32,4224]{1,0:T(8,128)(2,1)} %get-tuple-element.5.x_ref, f32[32,4096]{1,0:T(8,128)} %get-tuple-element.6.resid_ref, bf16[4096,896]{1,0:T(8,128)(2,1)} %bitcast.11, bf16[4096,896]{1,0:T(8,128)(2,1)} %bitcast.12, bf16[896,4096]{1,0:T(8,128)(2,1)} %bitcast.13), custom_call_target="tpu_custom_call" | custom-call | tf_op jit(solution)/shard_map/expert_layer/pallas_call | solution.py:788
  204.3 1.5 reshape.31
  205.8 1.7 copy.17

commit v5 on v4

--- a/solution.py
+++ b/solution.py
@@ -46,6 +46,7 @@
     gates_ref,
     x_ref,
     resid_ref,
+    rows_ref,
     fresh_ref,
     hfull,
     normed,
@@ -339,6 +340,14 @@
             at = pl.ds((g * per_group + h) * head_dim, head_dim)
             heads[:, at] = done[h * span : (h + 1) * span]
 
+    columns = [fresh_ref[:, pl.ds(j * head_dim, head_dim)] for j in range(four)]
+    rows_ref[...] = lax.dot_general(
+        perm4,
+        jnp.concatenate(columns, axis=0),
+        (((0,), (0,)), ((), ())),
+        preferred_element_type=f32,
+    ).astype(bf16)
+
     def wo_use(slot, buf):
         weights = buf.reshape(4 * wo_ref.shape[1], chip_cols)
         got = jnp.dot(heads[...], weights, preferred_element_type=f32)
@@ -465,11 +474,12 @@
         out_shape=(
             jax.ShapeDtypeStruct((block, width + LANES), bf16),
             jax.ShapeDtypeStruct((block, width), f32),
-            jax.ShapeDtypeStruct((span, four * head_dim), bf16),
+            jax.ShapeDtypeStruct((span * four, head_dim), bf16),
         ),
         in_specs=[vmem, vmem, hbm, smem, vmem, vmem, vmem, vmem, vmem, vmem],
         out_specs=(vmem, vmem, vmem),
         scratch_shapes=[
+            pltpu.VMEM((span, four * head_dim), bf16),
             pltpu.VMEM((2, span, wide_half), bf16),
             pltpu.VMEM((ring, span, chip_cols), bf16),
             pltpu.VMEM((ring, 4, chip_cols // 4, four * head_dim), bf16),
@@ -817,6 +827,22 @@
     )(x_wide, resid, w_gate, w_up, w_down)
 
 
+def results_kernel(mixed_ref, fresh_ref, mixed_out, fresh_out):
+    mixed_out[...] = mixed_ref[...]
+    fresh_out[...] = fresh_ref[...]
+
+
+def results(mixed, fresh):
+    vmem = pl.BlockSpec(memory_space=pltpu.VMEM)
+    return pl.pallas_call(
+        results_kernel,
+        out_shape=tuple(jax.ShapeDtypeStruct(v.shape, v.dtype) for v in (mixed, fresh)),
+        in_specs=[vmem, vmem],
+        out_specs=(vmem, vmem),
+        name="results",
+    )(mixed, fresh)
+
+
 def shards(
     hidden,
     queries,
@@ -836,7 +862,8 @@
         hidden, queries, cache, cache_lengths, wkv, wo, attn_gain, moe_gain, expert_ids, gates
     )
     mixed = expert_layer(x_wide, resid, w_gate[0], w_up[0], w_down[0])
-    fresh_key_value = fresh.reshape(fresh.shape[0], *wkv.shape[1:])
+    mixed, fresh = results(mixed, fresh)
+    fresh_key_value = fresh.reshape(hidden.shape[0], *wkv.shape[1:])
     return (mixed, fresh_key_value)
 
 

time: 208 us -> 206 us (level)
  local copies, waits for them, and re-layouts: 3.16 us -> 0 us
where the time goes in v5:
time: 206 us
  Pallas kernels  205 us (100%)
    pallas_call x1, Pallas kernels, expert_layer(): pl.pallas_call(functools.partial(expert_kernel, half), out_shape=jax.Shap...  106 us
    pallas_call x1, Pallas kernels, prelude(): pl.pallas_call(functools.partial(prelude_kernel, half, side), out_shape=(...  97 us

profile of v5, /device:TPU:69, one launch (start us, length us, event | category | flops | bytes accessed | tf_op | source)
XLA Modules:
  0.0 206.0 jit_solution(8431395040031789081)
XLA Ops:
  1.3 97.0 %prelude.1 = (bf16[32,4224]{1,0:T(8,128)(2,1)}, f32[32,4096]{1,0:T(8,128)}, bf16[256,128]{1,0:T(8,128)(2,1)}) custom-call(bf16[64,2048]{1,0:T(8,128)(2,1)} %hid_ref.1, bf16[2,256,128]{2,1,0:T(8,128)(2,1)} %bitcast.18, bf16[8192,128]{1,0:T(8,128)(2,1)} %bitcast.15, s32[1]{0:T(128)S(6)} %copy.15.len_ref, bf16[4,256,128]{2,1,0:T(8,128)(2,1)} %bitcast.17, ...), custom_call_target="tpu_custom_call" | custom-call | tf_op jit(solution)/shard_map/prelude/pallas_call | solution.py:472
  98.3 106.0 %expert_layer.1.mixed_ref = bf16[32,4096]{1,0:T(8,128)(2,1)} custom-call(bf16[32,4224]{1,0:T(8,128)(2,1)} %get-tuple-element.7.x_ref, f32[32,4096]{1,0:T(8,128)} %get-tuple-element.8.resid_ref, bf16[4096,896]{1,0:T(8,128)(2,1)} %bitcast.12, bf16[4096,896]{1,0:T(8,128)(2,1)} %bitcast.13, bf16[896,4096]{1,0:T(8,128)(2,1)} %bitcast.14), custom_call_target="tpu_custom_call" | custom-call | tf_op jit(solution)/shard_map/expert_layer/pallas_call | solution.py:798
  204.3 1.7 results.1

commit v6 on v5

--- a/solution.py
+++ b/solution.py
@@ -76,6 +76,10 @@
     won_recv,
     p_send,
     p_recv,
+    end_send,
+    end_recv,
+    endn_send,
+    endn_recv,
 ):
     ring = 2 * half
     z = lax.axis_index("tok")
@@ -156,6 +160,31 @@
             device_id_type=MESH,
         )
 
+    part_rows = wo_ref.shape[1] // 2
+
+    def end_copy(flow, sub):
+        q = quarters[flow]
+        at = pl.ds(sub * part_rows, part_rows)
+        return pltpu.make_async_remote_copy(
+            src_ref=wobuf.at[2 * (half - 1) + flow, q, at],
+            dst_ref=wobuf.at[1, q, at],
+            send_sem=end_send.at[flow, sub],
+            recv_sem=end_recv.at[flow, sub],
+            device_id={"tok": behind if flow == 0 else ahead},
+            device_id_type=MESH,
+        )
+
+    def end_side(axis, sub):
+        at = pl.ds(sub * part_rows, part_rows)
+        return pltpu.make_async_remote_copy(
+            src_ref=wobuf.at[1, own, at],
+            dst_ref=wobuf.at[1, own, at],
+            send_sem=endn_send.at[axis, sub],
+            recv_sem=endn_recv.at[axis, sub],
+            device_id=neighbours[axis],
+            device_id_type=MESH,
+        )
+
     def arrive(kind, step, pieces=(0, 1)):
         buf = kinds[kind][0]
         for piece in pieces:
@@ -167,7 +196,10 @@
                 ring_copy(kind, buf.at[slot], step, flow, piece).wait_recv()
                 if not final:
                     turn = isinstance(step, int) and step == half - 1
-                    if not turn or flow == piece:
+                    if turn and flow == piece and kind == "wo":
+                        for sub in range(2):
+                            end_copy(flow, sub).start()
+                    elif not turn or flow == piece:
                         ring_copy(kind, buf.at[slot], step + 1, flow, piece).start()
                 if piece == 0:
                     for axis in range(2):
@@ -403,11 +435,18 @@
         return carry
 
     lax.fori_loop(1, half - 3, early, 0)
-    arrive("wo", half)
+    for sub in range(2):
+        end_copy(0, sub).wait_recv()
+        for axis in range(2):
+            end_side(axis, sub).start()
+    for sub in range(2):
+        end_copy(1, sub).wait_recv()
     wo_settled(half - 2)
     wo_settled(half - 1)
     lax.fori_loop(half - 3, half, early, 0)
-    settle("wo", 1)
+    for sub in range(2):
+        for axis in range(2):
+            end_side(axis, sub).wait_recv()
     wo_use(1, wobuf[1])
     part_copy(0).start()
     part_copy(0).wait_recv()
@@ -434,9 +473,11 @@
         return carry
 
     lax.fori_loop(1, half, drain_ring, 0)
-    for kind in ("kv", "wo"):
-        for flow in range(2):
-            ring_copy(kind, kinds[kind][0].at[0], half, flow, flow).wait_send()
+    for flow in range(2):
+        ring_copy("kv", kvbuf.at[0], half, flow, flow).wait_send()
+        for sub in range(2):
+            end_copy(flow, sub).wait_send()
+            end_side(flow, sub).wait_send()
 
     def drain_sides(slot, carry):
         for kind in ("kv", "wo"):
@@ -444,7 +485,9 @@
                 side_copy(kind, slot, axis).wait_send()
         return carry
 
-    lax.fori_loop(1, ring, drain_sides, 0)
+    for axis in range(2):
+        side_copy("kv", 1, axis).wait_send()
+    lax.fori_loop(2, ring, drain_sides, 0)
 
     def drain_parts(g, carry):
         part_copy(g).wait_send()
@@ -508,6 +551,10 @@
             dma((ring, 2)),
             dma((half,)),
             dma((half,)),
+            dma((2, 2)),
+            dma((2, 2)),
+            dma((2, 2)),
+            dma((2, 2)),
         ],
         compiler_params=pltpu.CompilerParams(
             collective_id=0, has_side_effects=True, vmem_limit_bytes=67043328

time: 206 us -> 206 us (level)
  no operation moved by 1% of the time
where the time goes in v6:
time: 206 us
  Pallas kernels  205 us (100%)
    pallas_call x1, Pallas kernels, expert_layer(): pl.pallas_call(functools.partial(expert_kernel, half), out_shape=jax.Shap...  106 us
    pallas_call x1, Pallas kernels, prelude(): pl.pallas_call(functools.partial(prelude_kernel, half, side), out_shape=(...  97.2 us

profile of v6, /device:TPU:69, one launch (start us, length us, event | category | flops | bytes accessed | tf_op | source)
XLA Modules:
  0.0 206.2 jit_solution(18345573973915133375)
XLA Ops:
  1.3 97.2 %prelude.1 = (bf16[32,4224]{1,0:T(8,128)(2,1)}, f32[32,4096]{1,0:T(8,128)}, bf16[256,128]{1,0:T(8,128)(2,1)}) custom-call(bf16[64,2048]{1,0:T(8,128)(2,1)} %hid_ref.1, bf16[2,256,128]{2,1,0:T(8,128)(2,1)} %bitcast.18, bf16[8192,128]{1,0:T(8,128)(2,1)} %bitcast.15, s32[1]{0:T(128)S(6)} %copy.15.len_ref, bf16[4,256,128]{2,1,0:T(8,128)(2,1)} %bitcast.17, ...), custom_call_target="tpu_custom_call" | custom-call | tf_op jit(solution)/shard_map/prelude/pallas_call | solution.py:515
  98.5 106.0 %expert_layer.1.mixed_ref = bf16[32,4096]{1,0:T(8,128)(2,1)} custom-call(bf16[32,4224]{1,0:T(8,128)(2,1)} %get-tuple-element.7.x_ref, f32[32,4096]{1,0:T(8,128)} %get-tuple-element.8.resid_ref, bf16[4096,896]{1,0:T(8,128)(2,1)} %bitcast.12, bf16[4096,896]{1,0:T(8,128)(2,1)} %bitcast.13, bf16[896,4096]{1,0:T(8,128)(2,1)} %bitcast.14), custom_call_target="tpu_custom_call" | custom-call | tf_op jit(solution)/shard_map/expert_layer/pallas_call | solution.py:845
  204.5 1.7 results.1
